TPU v7x, 32 devices: a whole 2x2x4 slice. The times are simulated.
32 devices in a mesh: group: 2 (over y), blk: 4 (over z), uly: 4 (over x, core).
Axes of the slice: x: 2, y: 2, z: 4, core: 2. Of those that a mesh axis runs over, the one named last changes fastest.
Arguments:
- query: bfloat16 [768, 3072], P(('group', 'blk', 'uly')), parts along dimension 0, may hold values from -16 to 16
- keys: bfloat16 [768, 3072], P(('group', 'blk', 'uly')), parts along dimension 0, may hold values from -16 to 16
- values: bfloat16 [768, 3072], P(('group', 'blk', 'uly')), parts along dimension 0, may hold values from -6 to 6
- out_weight: bfloat16 [3072, 3072], P('uly', 'blk'), may hold values from -1 to 1
- out_gain: float32 [3072], replicated, may hold values from 0.1 to 1.9
Outputs:
- gated_out: bfloat16 [768, 3072], P(('group', 'blk', 'uly')), parts along dimension 0
There are 2 independent parts, one for each index of `group`. A program takes and returns all parts, laid end to end along the dimension named above; an argument that names none is the same for every part. Nothing has to cross between parts.
All inputs are finite; a program needn't handle non-finite values.
Results may differ from a plain program's by a relative error of at most 0.015.
Values may be sent and summed in bfloat16 or wider, within the bound.
A program may use at most 128 MiB of HBM per device.

v0:
```python
import functools
import math

import jax
import jax.numpy as jnp
from jax import lax
from jax.experimental import pallas as pl
from jax.experimental.pallas import tpu as pltpu
from jax.sharding import PartitionSpec as P

HEAD = 64
LANES = 128
MESH = pl.DeviceIdType.MESH

def make_fold(query_heads, state_now, pieces):
    score_scale = 1.0 / math.sqrt(HEAD)
    head_count = query_heads.shape[1]
    running_max, denominator, weighted = state_now
    key_part, value_part = pieces
    key_count = key_part.shape[0]
    key_heads = key_part.reshape(key_count, head_count, HEAD)
    value_heads = value_part.reshape(key_count, head_count, HEAD)
    scores = (
        jnp.einsum("qhd,khd->qhk", query_heads, key_heads, preferred_element_type=jnp.float32)
        * score_scale
    )
    new_max = jnp.max(scores, axis=2)
    weights = jnp.exp(scores - new_max[:, :, None])
    shrink = jnp.exp(running_max - new_max)
    denominator = denominator * shrink + jnp.sum(weights, axis=2)
    weighted = weighted * shrink[:, :, None] + jnp.einsum(
        "qhk,khd->qhd",
        weights.astype(jnp.bfloat16),
        value_heads,
        preferred_element_type=jnp.float32,
    )
    return (new_max, denominator, weighted)


def initial_state(row_count, head_count):
    return (
        jnp.full((row_count, head_count), -jnp.inf, jnp.float32),
        jnp.zeros((row_count, head_count), jnp.float32),
        jnp.zeros((row_count, head_count, HEAD), jnp.float32),
    )


def on_device(query, keys, values, out_weight, out_gain):
    grouped_q, grouped_k, grouped_v = (
        lax.all_to_all(query, "uly", split_axis=1, concat_axis=0, tiled=True),
        lax.all_to_all(keys, "uly", split_axis=1, concat_axis=0, tiled=True),
        lax.all_to_all(values, "uly", split_axis=1, concat_axis=0, tiled=True),
    )
    row_count = grouped_q.shape[0]
    features = grouped_q.shape[1]
    local_heads = features // HEAD
    query_heads = grouped_q.reshape(row_count, local_heads, HEAD)
    half_heads = local_heads // 2
    half_width = half_heads * HEAD
    low_state = make_fold(
        query_heads[:, :half_heads],
        initial_state(row_count, half_heads),
        (
            lax.all_gather(grouped_k[:, :half_width], "blk", axis=0, tiled=True),
            lax.all_gather(grouped_v[:, :half_width], "blk", axis=0, tiled=True),
        ),
    )
    high_state = make_fold(
        query_heads[:, half_heads:],
        initial_state(row_count, local_heads - half_heads),
        (
            lax.all_gather(grouped_k[:, half_width:], "blk", axis=0, tiled=True),
            lax.all_gather(grouped_v[:, half_width:], "blk", axis=0, tiled=True),
        ),
    )
    denominator = jnp.concatenate([low_state[1], high_state[1]], axis=1)
    weighted = jnp.concatenate([low_state[2], high_state[2]], axis=1)
    attended = (
        (weighted / denominator[:, :, None]).reshape(row_count, features).astype(jnp.bfloat16)
    )
    partial_value = jnp.dot(
        attended,
        lax.all_gather(out_weight, "blk", axis=1, tiled=True),
        preferred_element_type=jnp.float32,
    )
    summed = lax.psum_scatter(
        partial_value.astype(jnp.bfloat16), "uly", scatter_dimension=0, tiled=True
    ).astype(jnp.float32)
    return (out_gain * summed).astype(jnp.bfloat16)


def attend_kernel(
    nb, nu,
    q_hbm, k_hbm, v_hbm, w_hbm, gain_ref, out_ref,
    q_ref, k_ref, v_ref, stage_a, stage_b, got_a, got_b, w_ref,
    att_pair, att_one, att_all, part_f32, part_send, part_got, final_send,
    in_sem, send_a, send_b, recv_a, recv_b,
    send_p, recv_p, send_o, recv_o, pass_p, pass_o, send_r, recv_r, send_f, recv_f,
):
    n = nb * nu
    rows, width = q_ref.shape
    tokens = n * rows
    pairs = stage_a.shape[1] // 3
    heads = 2 * pairs + 1
    block = nu * rows
    half = block // 2
    side = nb // 2
    upper = (rows // 8 + 1) // 2 * 8
    scale = 1.0 / math.sqrt(HEAD)
    me_b, me_u = lax.axis_index("blk"), lax.axis_index("uly")
    me = me_b * nu + me_u
    my_side = me_b // side
    gate_here = (side - 1) + my_side
    gate_there = side - my_side
    is_gate = me_b == gate_here

    def turn_of(b, e):
        upward = b // side
        return upward * e + (1 - upward) * (nb - 1 - e)

    def there(b, u):
        return dict(device_id={"blk": b, "uly": u}, device_id_type=MESH)

    barrier = pltpu.get_barrier_semaphore()

    @pl.loop(1, n)
    def _(d):
        j = lax.rem(me + d, n)
        pl.semaphore_signal(barrier, inc=1, **there(j // nu, lax.rem(j, nu)))

    loads = [
        pltpu.make_async_copy(src, dst, in_sem.at[i])
        for i, (src, dst) in enumerate(
            ((q_hbm, q_ref), (k_hbm, k_ref), (v_hbm, v_ref), (w_hbm, w_ref)))
    ]
    for load in loads:
        load.start()
    for load in loads[:3]:
        load.wait()

    for c in range(n):
        odd = c % 2
        first = (heads * c - odd) // 2
        pair_at = first + odd
        one_at = first + (0 if odd else pairs)
        for s, ref in enumerate((q_ref, k_ref, v_ref)):
            for p in range(pairs):
                stage_a[c, s * pairs + p] = ref[:, pl.ds((pair_at + p) * LANES, LANES)]
        q_one, k_one, v_one = (
            ref[:, pl.ds(one_at * LANES, LANES)].astype(jnp.float32)[:, odd * HEAD:(odd + 1) * HEAD]
            for ref in (q_ref, k_ref, v_ref))
        rest = jnp.concatenate(
            [v_one[upper:], jnp.zeros((2 * upper - rows, HEAD), jnp.float32)]
            if 2 * upper > rows else [v_one[upper:]], axis=0)
        stage_b[c] = jnp.concatenate(
            [jnp.concatenate([q_one, k_one], axis=1), jnp.concatenate([v_one[:upper], rest], axis=1)],
            axis=0).astype(jnp.bfloat16)
    mine = me_u * nb + me_b
    got_a[me] = stage_a[mine]
    got_b[me] = stage_b[mine]

    pl.semaphore_wait(barrier, n - 1)

    def exchange(stage, got, send, recv, b, u):
        return pltpu.make_async_remote_copy(
            src_ref=stage.at[u * nb + b], dst_ref=got.at[me],
            send_sem=send.at[b * nu + u], recv_sem=recv.at[me], **there(b, u))

    def arrival(stage, got, send, recv, d):
        j = lax.rem(me + n - d, n)
        return pltpu.make_async_remote_copy(
            src_ref=stage.at[j], dst_ref=got.at[j],
            send_sem=send.at[j], recv_sem=recv.at[j], **there(me_b, me_u))

    a_refs = (stage_a, got_a, send_a, recv_a)
    b_refs = (stage_b, got_b, send_b, recv_b)

    for refs in (a_refs, b_refs):
        for d in range(n - 1, 0, -1):
            exchange(*refs, lax.rem(me_b + d // nu, nb), lax.rem(me_u + d % nu, nu)).start()

    @pl.loop(1, n)
    def _(d):
        arrival(*a_refs, d).wait_recv()

    def softmax(scores):
        scores = scores * scale
        top = jnp.max(scores, axis=1, keepdims=True)
        weights = jnp.exp(scores - top)
        return weights.astype(jnp.bfloat16), jnp.sum(weights, axis=1, keepdims=True)

    def against(a, b):
        return lax.dot_general(a, b, (((1,), (1,)), ((), ())), preferred_element_type=jnp.float32)

    wide_low = lax.broadcasted_iota(jnp.int32, (tokens, LANES), 1) < HEAD

    def whole(ref, s):
        return jnp.concatenate([ref[i, s].astype(jnp.float32) for i in range(n)], axis=0)

    for p in range(pairs):
        q_all = whole(got_a, p)
        k_all = whole(got_a, pairs + p).astype(jnp.bfloat16)
        v_all = whole(got_a, 2 * pairs + p).astype(jnp.bfloat16)
        pieces = []
        for keep in (wide_low, jnp.logical_not(wide_low)):
            q_one = jnp.where(keep, q_all, 0.0).astype(jnp.bfloat16)
            weights, total = softmax(against(q_one, k_all))
            pieces.append(jnp.dot(weights, v_all, preferred_element_type=jnp.float32) / total)
        joined = jnp.where(wide_low, *pieces).astype(jnp.bfloat16)
        for t in range(nb):
            att_pair[me_b, t, p] = joined[t * block:(t + 1) * block]

    def target(d):
        return gate_there if d == 0 else my_side * side + lax.rem(me_b + d, side)

    def spread(ref, send, recv, d, e):
        t = turn_of(target(d), e)
        return pltpu.make_async_remote_copy(
            src_ref=ref.at[me_b, t], dst_ref=ref.at[me_b, t],
            send_sem=send.at[d, t], recv_sem=recv.at[me_b, t], **there(target(d), me_u))

    def spread_in(ref, send, recv, b, t):
        return pltpu.make_async_remote_copy(
            src_ref=ref.at[b, t], dst_ref=ref.at[b, t],
            send_sem=send.at[0, t], recv_sem=recv.at[b, t], **there(me_b, me_u))

    def pass_on(ref, sems, recv, d, far, t):
        return pltpu.make_async_remote_copy(
            src_ref=ref.at[far, t], dst_ref=ref.at[far, t],
            send_sem=sems.at[d, far, t], recv_sem=recv.at[far, t], **there(target(d), me_u))

    pair_refs, one_refs = (att_pair, send_p, recv_p), (att_one, send_o, recv_o)
    plan = [(0, e) for e in range(side)] + [(1, e) for e in range(side)]
    plan += [(kind, e) for e in range(side, nb) for kind in (0, 1)]
    both = ((*pair_refs, pass_p), (*one_refs, pass_o))
    for kind, e in plan[:side]:
        for d in range(side):
            spread(*both[kind][:3], d, e).start()

    @pl.loop(1, n)
    def _(d):
        arrival(*b_refs, d).wait_recv()

    got = [got_b[i].astype(jnp.float32) for i in range(n)]
    qk_all = jnp.concatenate([g[:rows] for g in got], axis=0)
    v_all = jnp.concatenate(
        [piece for g in got
         for piece in (g[rows:, :HEAD], g[rows:2 * rows - upper, HEAD:])], axis=0)
    weights, total = softmax(
        against(qk_all[:, :HEAD].astype(jnp.bfloat16), qk_all[:, HEAD:].astype(jnp.bfloat16)))
    single = jnp.dot(
        weights, v_all.astype(jnp.bfloat16), preferred_element_type=jnp.float32) / total
    for t in range(nb):
        at = t * block
        att_one[me_b, t] = jnp.concatenate(
            [single[at:at + half], single[at + half:at + block]], axis=1).astype(jnp.bfloat16)
    for kind, e in plan[side:]:
        for d in range(side):
            spread(*both[kind][:3], d, e).start()

    def scatter(to, d):
        u = lax.rem(me_u + d, nu)
        return pltpu.make_async_remote_copy(
            src_ref=part_send.at[to, u], dst_ref=part_got.at[to, me_u],
            send_sem=send_r.at[to, d], recv_sem=recv_r.at[to, me_u], **there(me_b, u))

    def scatter_in(to, d):
        u = lax.rem(me_u + nu - d, nu)
        return pltpu.make_async_remote_copy(
            src_ref=part_send.at[to, u], dst_ref=part_got.at[to, u],
            send_sem=send_r.at[to, d], recv_sem=recv_r.at[to, u], **there(me_b, me_u))

    def final(to):
        return pltpu.make_async_remote_copy(
            src_ref=final_send.at[to], dst_ref=out_ref.at[me_b],
            send_sem=send_f.at[to], recv_sem=recv_f.at[me_b], **there(to, me_u))

    def final_in(d):
        b = lax.rem(me_b + nb - d, nb)
        return pltpu.make_async_remote_copy(
            src_ref=final_send.at[b], dst_ref=out_ref.at[b],
            send_sem=send_f.at[b], recv_sem=recv_f.at[b], **there(me_b, me_u))

    def reduce(e):
        to = turn_of(me_b, e)
        total = part_f32[to, me_u]
        for d in range(1, nu):
            scatter_in(to, d).wait_recv()
            total += part_got[to, lax.rem(me_u + nu - d, nu)].astype(jnp.float32)
        gated = (gain_ref[me_b] * total).astype(jnp.bfloat16)

        @pl.when(me_b == to)
        def _():
            out_ref[to] = gated

        @pl.when(me_b != to)
        def _():
            final_send[to] = gated
            final(to).start()

    loads[3].wait()
    far_side = (1 - my_side) * side
    for kind, turn in plan:
        t = turn_of(me_b, turn)
        ref, send, recv, passed = both[kind]
        for i in range(side):
            far = far_side + i
            spread_in(ref, send, recv, far, t).wait_recv()

            @pl.when(is_gate)
            def _():
                for d in range(1, side):
                    pass_on(ref, passed, recv, d, far, t).start()
        if kind == 0:
            continue
        for d in range(1, side):
            near = target(d)
            spread_in(*pair_refs, near, t).wait_recv()
            spread_in(*one_refs, near, t).wait_recv()
        for b in range(0, nb, 2):
            tile = heads * b // 2
            for p in range(pairs):
                att_all[:, pl.ds((tile + p) * LANES, LANES)] = att_pair[b, t, p]
                att_all[:, pl.ds((tile + pairs + 1 + p) * LANES, LANES)] = att_pair[b + 1, t, p]
            even, odd = att_one[b, t].astype(jnp.float32), att_one[b + 1, t].astype(jnp.float32)
            at = pl.ds((tile + pairs) * LANES, LANES)
            att_all[:, at] = jnp.concatenate(
                [jnp.concatenate([even[:, :HEAD], odd[:, :HEAD]], axis=1),
                 jnp.concatenate([even[:, HEAD:], odd[:, HEAD:]], axis=1)],
                axis=0).astype(jnp.bfloat16)
        part = jnp.dot(att_all[...], w_ref[...], preferred_element_type=jnp.float32)
        for u in range(nu):
            one = part[u * rows:(u + 1) * rows]
            part_f32[t, u] = one
            part_send[t, u] = one.astype(jnp.bfloat16)
        for d in range(1, nu):
            scatter(t, d).start()
        if turn >= 2:
            reduce(turn - 2)
    for turn in range(nb - 2, nb):
        reduce(turn)

    for d in range(1, nb):
        final_in(d).wait_recv()

    @pl.loop(1, n)
    def _(d):
        j = lax.rem(me + d, n)
        exchange(*a_refs, j // nu, lax.rem(j, nu)).wait_send()
        exchange(*b_refs, j // nu, lax.rem(j, nu)).wait_send()

    for t in range(nb):
        for d in range(side):
            spread(*pair_refs, d, t).wait_send()
            spread(*one_refs, d, t).wait_send()
        for d in range(1, nu):
            scatter(t, d).wait_send()

        @pl.when(me_b != t)
        def _():
            final(t).wait_send()

        @pl.when(is_gate)
        def _():
            for i in range(side):
                for d in range(1, side):
                    pass_on(att_pair, pass_p, recv_p, d, far_side + i, t).wait_send()
                    pass_on(att_one, pass_o, recv_o, d, far_side + i, t).wait_send()


def fused(nb, nu, query, keys, values, out_weight, out_gain):
    n = nb * nu
    rows, width = query.shape
    heads = width // HEAD // n
    pairs = heads // 2
    depth, columns = out_weight.shape
    bf16, f32 = jnp.bfloat16, jnp.float32
    vmem, dma = pltpu.VMEM, pltpu.SemaphoreType.DMA
    in_vmem = pl.BlockSpec(memory_space=pltpu.VMEM)
    in_place = pl.BlockSpec(memory_space=pl.ANY)
    block, side = nu * rows, nb // 2
    upper = (rows // 8 + 1) // 2 * 8
    gathered = pl.pallas_call(
        functools.partial(attend_kernel, nb, nu),
        out_shape=jax.ShapeDtypeStruct((nb, rows, columns), bf16),
        in_specs=[in_place, in_place, in_place, in_place, in_vmem],
        out_specs=in_vmem,
        scratch_shapes=[
            vmem((rows, width), bf16), vmem((rows, width), bf16), vmem((rows, width), bf16),
            vmem((n, 3 * pairs, rows, LANES), bf16),
            vmem((n, rows + upper, LANES), bf16),
            vmem((n, 3 * pairs, rows, LANES), bf16),
            vmem((n, rows + upper, LANES), bf16),
            vmem((depth, columns), bf16),
            vmem((nb, nb, pairs, block, LANES), bf16),
            vmem((nb, nb, block // 2, LANES), bf16),
            vmem((block, depth), bf16),
            vmem((nb, nu, rows, columns), f32),
            vmem((nb, nu, rows, columns), bf16),
            vmem((nb, nu, rows, columns), bf16),
            vmem((nb, rows, columns), bf16),
            dma((4,)), dma((n,)), dma((n,)), dma((n,)), dma((n,)),
            dma((side, nb)), dma((nb, nb)), dma((side, nb)), dma((nb, nb)),
            dma((side, nb, nb)), dma((side, nb, nb)),
            dma((nb, nu)), dma((nb, nu)), dma((nb,)), dma((nb,)),
        ],
        compiler_params=pltpu.CompilerParams(collective_id=0, has_side_effects=True),
    )(query, keys, values, out_weight, out_gain.reshape(nb, 1, columns))
    return gathered.transpose(1, 0, 2).reshape(rows, width)


def on_any(nb, nu, query, keys, values, out_weight, out_gain):
    n = nb * nu
    rows, width = query.shape
    heads = width // HEAD
    suits = (
        heads % n == 0 and (heads // n) % 2 == 1 and heads // n > 1 and nb % 2 == 0
        and rows % 8 == 0 and (width // nb) % LANES == 0
    )
    plan = functools.partial(fused, nb, nu) if suits else on_device
    return plan(query, keys, values, out_weight, out_gain)


def solution(mesh):
    in_specs = (
        P(("group", "blk", "uly"), None),
        P(("group", "blk", "uly"), None),
        P(("group", "blk", "uly"), None),
        P("uly", "blk"),
        P(),
    )
    out_specs = P(("group", "blk", "uly"), None)
    body = functools.partial(on_any, mesh.shape["blk"], mesh.shape["uly"])
    return jax.shard_map(
        body, mesh=mesh, in_specs=in_specs, out_specs=out_specs, check_vma=False
    )
```

profile of v0, /device:TPU:0, one launch (start us, length us, event | category | flops | bytes accessed | tf_op | source)
XLA Modules:
  0.0 39.1 jit_solution(207866356974709982)
XLA Ops:
  0.0 37.5 %shard_map.55 = bf16[4,24,768]{2,1,0:T(8,128)(2,1)} custom-call(bf16[24,3072]{1,0:T(8,128)(2,1)} %q_hbm.1, bf16[24,3072]{1,0:T(8,128)(2,1)} %k_hbm.1, bf16[24,3072]{1,0:T(8,128)(2,1)} %v_hbm.1, bf16[768,768]{1,0:T(8,128)(2,1)} %w_hbm.1, f32[4,1,768]{2,1,0:T(1,128)} %bitcast.5), custom_call_target="tpu_custom_call" | custom-call | tf_op jit(solution)/shard_map/pallas_call | solution.py:383
  37.5 1.6 %copy.7 = bf16[4,3,8,768]{3,2,0,1:T(8,128)(2,1)} copy(bf16[4,3,8,768]{3,2,1,0:T(8,128)(2,1)} %bitcast.4) | data formatting | bytes 294912 | tf_op jit(solution)/shard_map/reshape | solution.py:409
where the time goes:
time: 39.3 us; the launch traced here: 39.1 us
  Pallas kernels  37.5 us (95%)
  local copies, waits for them, and re-layouts  1.58 us (4%)
    pallas_call x1, Pallas kernels, fused(): pl.pallas_call(functools.partial(attend_kernel, nb, nu), out_shape=jax.Sh...  37.5 us
    reshape x1, local copies, waits for them, and re-layouts, fused(): return gathered.transpose(1, 0, 2).reshape(rows, width)  1.58 us

commit v1 on v0

v1 whole, which is shorter than its diff:
```python
import functools
import math

import jax
import jax.numpy as jnp
from jax import lax
from jax.experimental import pallas as pl
from jax.experimental.pallas import tpu as pltpu
from jax.sharding import PartitionSpec as P

HEAD = 64
LANES = 128
MESH = pl.DeviceIdType.MESH

def make_fold(query_heads, state_now, pieces):
    score_scale = 1.0 / math.sqrt(HEAD)
    head_count = query_heads.shape[1]
    running_max, denominator, weighted = state_now
    key_part, value_part = pieces
    key_count = key_part.shape[0]
    key_heads = key_part.reshape(key_count, head_count, HEAD)
    value_heads = value_part.reshape(key_count, head_count, HEAD)
    scores = (
        jnp.einsum("qhd,khd->qhk", query_heads, key_heads, preferred_element_type=jnp.float32)
        * score_scale
    )
    new_max = jnp.max(scores, axis=2)
    weights = jnp.exp(scores - new_max[:, :, None])
    shrink = jnp.exp(running_max - new_max)
    denominator = denominator * shrink + jnp.sum(weights, axis=2)
    weighted = weighted * shrink[:, :, None] + jnp.einsum(
        "qhk,khd->qhd",
        weights.astype(jnp.bfloat16),
        value_heads,
        preferred_element_type=jnp.float32,
    )
    return (new_max, denominator, weighted)


def initial_state(row_count, head_count):
    return (
        jnp.full((row_count, head_count), -jnp.inf, jnp.float32),
        jnp.zeros((row_count, head_count), jnp.float32),
        jnp.zeros((row_count, head_count, HEAD), jnp.float32),
    )


def on_device(query, keys, values, out_weight, out_gain):
    grouped_q, grouped_k, grouped_v = (
        lax.all_to_all(query, "uly", split_axis=1, concat_axis=0, tiled=True),
        lax.all_to_all(keys, "uly", split_axis=1, concat_axis=0, tiled=True),
        lax.all_to_all(values, "uly", split_axis=1, concat_axis=0, tiled=True),
    )
    row_count = grouped_q.shape[0]
    features = grouped_q.shape[1]
    local_heads = features // HEAD
    query_heads = grouped_q.reshape(row_count, local_heads, HEAD)
    half_heads = local_heads // 2
    half_width = half_heads * HEAD
    low_state = make_fold(
        query_heads[:, :half_heads],
        initial_state(row_count, half_heads),
        (
            lax.all_gather(grouped_k[:, :half_width], "blk", axis=0, tiled=True),
            lax.all_gather(grouped_v[:, :half_width], "blk", axis=0, tiled=True),
        ),
    )
    high_state = make_fold(
        query_heads[:, half_heads:],
        initial_state(row_count, local_heads - half_heads),
        (
            lax.all_gather(grouped_k[:, half_width:], "blk", axis=0, tiled=True),
            lax.all_gather(grouped_v[:, half_width:], "blk", axis=0, tiled=True),
        ),
    )
    denominator = jnp.concatenate([low_state[1], high_state[1]], axis=1)
    weighted = jnp.concatenate([low_state[2], high_state[2]], axis=1)
    attended = (
        (weighted / denominator[:, :, None]).reshape(row_count, features).astype(jnp.bfloat16)
    )
    partial_value = jnp.dot(
        attended,
        lax.all_gather(out_weight, "blk", axis=1, tiled=True),
        preferred_element_type=jnp.float32,
    )
    summed = lax.psum_scatter(
        partial_value.astype(jnp.bfloat16), "uly", scatter_dimension=0, tiled=True
    ).astype(jnp.float32)
    return (out_gain * summed).astype(jnp.bfloat16)


def attend_kernel(
    nb, nu,
    q_hbm, k_hbm, v_hbm, w_hbm, gain_ref, out_ref,
    q_ref, k_ref, v_ref, stage, got, far, w_ref,
    att, acc, part_f32, part_send, part_got, final_send,
    in_sem, w_sem, send_a, recv_a, send_k, recv_k, up_sem,
    send_b, recv_b, pass_b, send_r, recv_r, send_f, recv_f,
):
    nx = nu // 2
    m = nb * nx
    rows, width = q_ref.shape
    pairs = stage.shape[1]
    last = pairs - 1
    depth = w_hbm.shape[0]
    block = nx * rows
    mine_rows = nb * block
    side = nb // 2
    scale = math.log2(math.e) / math.sqrt(HEAD)
    me_b, me_u = lax.axis_index("blk"), lax.axis_index("uly")
    me_x, me_c = me_u // 2, lax.rem(me_u, 2)
    me = me_b * nx + me_x
    my_side = me_b // side
    gate_here = (side - 1) + my_side
    gate_there = side - my_side
    is_gate = me_b == gate_here
    far_side = (1 - my_side) * side

    def turn_of(b, e):
        upward = b // side
        return upward * e + (1 - upward) * (nb - 1 - e)

    def there(b, x):
        return dict(device_id={"blk": b, "uly": 2 * x + me_c}, device_id_type=MESH)

    partner = dict(device_id={"blk": me_b, "uly": 2 * me_x + 1 - me_c}, device_id_type=MESH)
    barrier = pltpu.get_barrier_semaphore()

    pl.semaphore_signal(barrier, inc=1, **partner)
    for d in range(1, nx):
        pl.semaphore_signal(barrier, inc=1, **there(me_b, lax.rem(me_x + d, nx)))
    for b in range(1, nb):

        @pl.when(b > me_b)
        def _():
            for x in range(nx):
                pl.semaphore_signal(barrier, inc=1, **there(b, x))

    loads = [
        pltpu.make_async_copy(src, dst, in_sem.at[i])
        for i, (src, dst) in enumerate(
            ((q_hbm, q_ref), (k_hbm, k_ref), (v_hbm, v_ref),
             (w_hbm, w_ref.at[pl.ds(pl.multiple_of(me_c * depth, depth), depth)])))
    ]
    for load in loads[:3]:
        load.start()
    for load in loads[:3]:
        load.wait()
    loads[3].start()

    for b in range(nb):
        for x in range(nx):
            for p in range(pairs):
                at = ((x * nb + b) * pairs + p) * LANES
                for s, ref in enumerate((q_ref, k_ref, v_ref)):
                    stage[b * nx + x, p, s] = ref[:, pl.ds(at, LANES)]
    for p in range(pairs):
        for s in range(3):
            got[p, s, me] = stage[me, p, s]

    pl.semaphore_wait(barrier, me_b * nx + nx)
    for b in range(nb - 1):

        @pl.when(b < me_b)
        def _():
            for x in range(nx):
                pl.semaphore_signal(up_sem.at[me_b], inc=1, **there(b, x))

    def ship(p, b, x):
        return pltpu.make_async_remote_copy(
            src_ref=stage.at[b * nx + x, p], dst_ref=got.at[p, :, me],
            send_sem=send_a.at[p, b * nx + x], recv_sem=recv_a.at[p, me], **there(b, x))

    def shipped(p, j):
        return pltpu.make_async_remote_copy(
            src_ref=stage.at[j, p], dst_ref=got.at[p, :, j],
            send_sem=send_a.at[p, j], recv_sem=recv_a.at[p, j], **there(me_b, me_x))

    def ship_level(p, b):
        for d in range(nx - 1, -1, -1):
            ship(p, b, lax.rem(me_x + d, nx)).start()

    for p in range(pairs):
        for b in range(nb - 1):

            @pl.when(b < me_b)
            def _():
                ship_level(p, b)
        for d in range(1, nx):
            ship(p, me_b, lax.rem(me_x + d, nx)).start()

    w_swap = pltpu.make_async_remote_copy(
        src_ref=w_hbm, dst_ref=w_ref.at[pl.ds(pl.multiple_of(me_c * depth, depth), depth)],
        send_sem=w_sem.at[0], recv_sem=w_sem.at[1], **partner)
    w_swap.start()

    for b in range(1, nb):

        @pl.when(b > me_b)
        def _():
            pl.semaphore_wait(up_sem.at[b], nx)
            for p in range(last):
                ship_level(p, b)
    for b in range(nb - 1, 0, -1):

        @pl.when(b > me_b)
        def _():
            ship_level(last, b)

    def swap(p):
        return pltpu.make_async_remote_copy(
            src_ref=got.at[p, pl.ds(1, 2)], dst_ref=far.at[p],
            send_sem=send_k.at[p], recv_sem=recv_k.at[p], **partner)

    def against(a, b):
        return lax.dot_general(a, b, (((1,), (1,)), ((), ())), preferred_element_type=jnp.float32)

    low = lax.broadcasted_iota(jnp.int32, (mine_rows, LANES), 1) < HEAD

    def target(d):
        return gate_there if d == 0 else my_side * side + lax.rem(me_b + d, side)

    def piece(ref, p, b, t):
        return ref.at[p, b] if p < last else ref.at[p, b, t]

    def spread(p, d, e):
        t = turn_of(target(d), e)
        slot = t if p == last else 0
        return pltpu.make_async_remote_copy(
            src_ref=piece(att, p, me_b, t), dst_ref=piece(att, p, me_b, t),
            send_sem=send_b.at[p, d, slot], recv_sem=recv_b.at[p, me_b, slot],
            **there(target(d), me_x))

    def spread_in(p, b, t):
        slot = t if p == last else 0
        return pltpu.make_async_remote_copy(
            src_ref=piece(att, p, b, t), dst_ref=piece(att, p, b, t),
            send_sem=send_b.at[p, 0, slot], recv_sem=recv_b.at[p, b, slot], **there(me_b, me_x))

    def pass_on(p, d, b, t):
        slot = t if p == last else 0
        return pltpu.make_async_remote_copy(
            src_ref=piece(att, p, b, t), dst_ref=piece(att, p, b, t),
            send_sem=pass_b.at[p, d, b, slot], recv_sem=recv_b.at[p, b, slot],
            **there(target(d), me_x))

    def parts_of(p):
        return range(nb) if p == last else range(1)

    for p in range(pairs):

        @pl.loop(1, m)
        def _(d):
            shipped(p, lax.rem(me + m - d, m)).wait_recv()

        swap(p).start()
        q_all = jnp.concatenate([got[p, 0, i].astype(jnp.float32) for i in range(m)], axis=0)
        q_two = jnp.concatenate(
            [jnp.where(low, q_all, 0.0), jnp.where(low, 0.0, q_all)], axis=0).astype(jnp.bfloat16)
        swap(p).wait_recv()
        k_all, v_all = (
            jnp.concatenate(
                [got[p, s, i].astype(jnp.float32) for i in range(m)]
                + [far[p, s - 1, i].astype(jnp.float32) for i in range(m)], axis=0
            ).astype(jnp.bfloat16)
            for s in (1, 2))
        scores = against(q_two, k_all)
        top = jnp.max(scores, axis=1, keepdims=True)
        weights = jnp.exp2((scores - top) * scale)
        total = jnp.sum(weights, axis=1, keepdims=True)
        both = jnp.dot(
            weights.astype(jnp.bfloat16), v_all, preferred_element_type=jnp.float32) / total
        joined = jnp.where(low, both[:mine_rows], both[mine_rows:]).astype(jnp.bfloat16)
        for t in range(nb):
            att[p, me_b, t] = joined[t * block:(t + 1) * block]
        for e in parts_of(p):
            for d in range(side):
                spread(p, d, e).start()

    def forward(p, t):
        for i in range(side):
            b = far_side + i
            spread_in(p, b, t).wait_recv()

            @pl.when(is_gate)
            def _():
                for d in range(1, side):
                    pass_on(p, d, b, t).start()

    def settle(p, t):
        forward(p, t)
        for d in range(1, side):
            spread_in(p, target(d), t).wait_recv()

    def weight_of(p):
        return jnp.concatenate(
            [w_ref[pl.ds((b * pairs + p) * LANES, LANES)] for b in range(nb)], axis=0)

    loads[3].wait()
    w_swap.wait_recv()
    for p in range(last):
        settle(p, 0)
        seen = jnp.concatenate(
            [att[p, b].reshape(mine_rows, LANES) for b in range(nb)], axis=1)
        part = jnp.dot(seen, weight_of(p), preferred_element_type=jnp.float32)
        part = part.reshape(acc.shape)
        if p == 0:
            acc[...] = part
        else:
            acc[...] += part

    def scatter(t, d):
        x = lax.rem(me_x + d, nx)
        return pltpu.make_async_remote_copy(
            src_ref=part_send.at[t, x], dst_ref=part_got.at[t, me_x],
            send_sem=send_r.at[t, d], recv_sem=recv_r.at[t, me_x], **there(me_b, x))

    def scatter_in(t, d):
        x = lax.rem(me_x + nx - d, nx)
        return pltpu.make_async_remote_copy(
            src_ref=part_send.at[t, x], dst_ref=part_got.at[t, x],
            send_sem=send_r.at[t, d], recv_sem=recv_r.at[t, x], **there(me_b, me_x))

    def final(t):
        return pltpu.make_async_remote_copy(
            src_ref=final_send.at[t], dst_ref=out_ref.at[me_b],
            send_sem=send_f.at[t], recv_sem=recv_f.at[me_b], **there(t, me_x))

    def final_in(d):
        b = lax.rem(me_b + nb - d, nb)
        return pltpu.make_async_remote_copy(
            src_ref=final_send.at[b], dst_ref=out_ref.at[b],
            send_sem=send_f.at[b], recv_sem=recv_f.at[b], **there(me_b, me_x))

    def reduce(e):
        t = turn_of(me_b, e)
        total = part_f32[t, me_x]
        for d in range(1, nx):
            scatter_in(t, d).wait_recv()
            total += part_got[t, lax.rem(me_x + nx - d, nx)].astype(jnp.float32)
        gated = (gain_ref[me_b] * total).astype(jnp.bfloat16)

        @pl.when(me_b == t)
        def _():
            out_ref[t] = gated

        @pl.when(me_b != t)
        def _():
            final_send[t] = gated
            final(t).start()

    lag = 2
    for e in range(nb):
        t = turn_of(me_b, e)
        settle(last, t)
        seen = jnp.concatenate([att[last, b, t] for b in range(nb)], axis=1)
        part = jnp.dot(seen, weight_of(last), preferred_element_type=jnp.float32)
        if pairs > 1:
            part += acc[t]
        for x in range(nx):
            one = part[x * rows:(x + 1) * rows]
            part_f32[t, x] = one
            part_send[t, x] = one.astype(jnp.bfloat16)
        for d in range(1, nx):
            scatter(t, d).start()
        if e >= lag:
            reduce(e - lag)
    for e in range(nb - lag, nb):
        reduce(e)

    for d in range(1, nb):
        final_in(d).wait_recv()

    w_swap.wait_send()
    for p in range(pairs):
        swap(p).wait_send()

        @pl.loop(1, m)
        def _(d):
            shipped(p, lax.rem(me + d, m)).wait_send()

        for e in parts_of(p):
            for d in range(side):
                spread(p, d, e).wait_send()

            @pl.when(is_gate)
            def _():
                for i in range(side):
                    for d in range(1, side):
                        pass_on(p, d, far_side + i, e).wait_send()
    for t in range(nb):
        for d in range(1, nx):
            scatter(t, d).wait_send()

        @pl.when(me_b != t)
        def _():
            final(t).wait_send()


def fused(nb, nu, query, keys, values, out_weight, out_gain):
    nx = nu // 2
    m = nb * nx
    rows, width = query.shape
    pairs = width // LANES // m
    depth, columns = out_weight.shape
    bf16, f32 = jnp.bfloat16, jnp.float32
    vmem, dma = pltpu.VMEM, pltpu.SemaphoreType.DMA
    in_vmem = pl.BlockSpec(memory_space=pltpu.VMEM)
    in_place = pl.BlockSpec(memory_space=pl.ANY)
    block, side = nx * rows, nb // 2
    gathered = pl.pallas_call(
        functools.partial(attend_kernel, nb, nu),
        out_shape=jax.ShapeDtypeStruct((nb, rows, columns), bf16),
        in_specs=[in_place, in_place, in_place, in_place, in_vmem],
        out_specs=in_vmem,
        scratch_shapes=[
            vmem((rows, width), bf16), vmem((rows, width), bf16), vmem((rows, width), bf16),
            vmem((m, pairs, 3, rows, LANES), bf16),
            vmem((pairs, 3, m, rows, LANES), bf16),
            vmem((pairs, 2, m, rows, LANES), bf16),
            vmem((2 * depth, columns), bf16),
            vmem((pairs, nb, nb, block, LANES), bf16),
            vmem((nb, block, columns), f32),
            vmem((nb, nx, rows, columns), f32),
            vmem((nb, nx, rows, columns), bf16),
            vmem((nb, nx, rows, columns), bf16),
            vmem((nb, rows, columns), bf16),
            dma((4,)), dma((2,)), dma((pairs, m)), dma((pairs, m)), dma((pairs,)), dma((pairs,)),
            pltpu.SemaphoreType.REGULAR((nb,)),
            dma((pairs, side, nb)), dma((pairs, nb, nb)), dma((pairs, side, nb, nb)),
            dma((nb, nx)), dma((nb, nx)), dma((nb,)), dma((nb,)),
        ],
        compiler_params=pltpu.CompilerParams(collective_id=0, has_side_effects=True),
    )(query, keys, values, out_weight, out_gain.reshape(nb, 1, columns))
    return gathered.transpose(1, 0, 2).reshape(rows, width)


def on_any(nb, nu, query, keys, values, out_weight, out_gain):
    rows, width = query.shape
    suits = (
        nu % 2 == 0 and nb % 2 == 0 and width % (LANES * nb * nu // 2) == 0
        and rows % 8 == 0 and (nu // 2 * rows) % 16 == 0 and (width // nb) % LANES == 0
    )
    plan = functools.partial(fused, nb, nu) if suits else on_device
    return plan(query, keys, values, out_weight, out_gain)


def solution(mesh):
    in_specs = (
        P(("group", "blk", "uly"), None),
        P(("group", "blk", "uly"), None),
        P(("group", "blk", "uly"), None),
        P("uly", "blk"),
        P(),
    )
    out_specs = P(("group", "blk", "uly"), None)
    body = functools.partial(on_any, mesh.shape["blk"], mesh.shape["uly"])
    return jax.shard_map(
        body, mesh=mesh, in_specs=in_specs, out_specs=out_specs, check_vma=False
    )
```

time: 39.3 us -> 40.9 us (1.041)
  Pallas kernels: 37.5 us -> 39.1 us
    pallas_call x1, Pallas kernels: 37.5 us -> 39.1 us  [fused(): pl.pallas_call(functools.partial(attend_kernel, nb, nu), out_shape=jax.Sh...]
where the time goes in v1:
time: 40.9 us; the launch traced here: 40.7 us
  Pallas kernels  39.1 us (96%)
  local copies, waits for them, and re-layouts  1.58 us (4%)
    pallas_call x1, Pallas kernels, fused(): pl.pallas_call(functools.partial(attend_kernel, nb, nu), out_shape=jax.Sh...  39.1 us
    reshape x1, local copies, waits for them, and re-layouts, fused(): return gathered.transpose(1, 0, 2).reshape(rows, width)  1.58 us

profile of v1, /device:TPU:0, one launch (start us, length us, event | category | flops | bytes accessed | tf_op | source)
XLA Modules:
  0.0 40.7 jit_solution(2444631532778989438)
XLA Ops:
  0.0 39.1 %shard_map.55 = bf16[4,24,768]{2,1,0:T(8,128)(2,1)} custom-call(bf16[24,3072]{1,0:T(8,128)(2,1)} %q_hbm.1, bf16[24,3072]{1,0:T(8,128)(2,1)} %k_hbm.1, bf16[24,3072]{1,0:T(8,128)(2,1)} %v_hbm.1, bf16[768,768]{1,0:T(8,128)(2,1)} %w_hbm.1, f32[4,1,768]{2,1,0:T(1,128)} %bitcast.5), custom_call_target="tpu_custom_call" | custom-call | tf_op jit(solution)/shard_map/pallas_call | solution.py:411
  39.1 1.6 %copy.7 = bf16[4,3,8,768]{3,2,0,1:T(8,128)(2,1)} copy(bf16[4,3,8,768]{3,2,1,0:T(8,128)(2,1)} %bitcast.4) | data formatting | bytes 294912 | tf_op jit(solution)/shard_map/reshape | solution.py:435

commit v2 on v1

v2 whole, which is shorter than its diff:
```python
import functools
import math

import jax
import jax.numpy as jnp
from jax import lax
from jax.experimental import pallas as pl
from jax.experimental.pallas import tpu as pltpu
from jax.sharding import PartitionSpec as P

HEAD = 64
LANES = 128
MESH = pl.DeviceIdType.MESH

def make_fold(query_heads, state_now, pieces):
    score_scale = 1.0 / math.sqrt(HEAD)
    head_count = query_heads.shape[1]
    running_max, denominator, weighted = state_now
    key_part, value_part = pieces
    key_count = key_part.shape[0]
    key_heads = key_part.reshape(key_count, head_count, HEAD)
    value_heads = value_part.reshape(key_count, head_count, HEAD)
    scores = (
        jnp.einsum("qhd,khd->qhk", query_heads, key_heads, preferred_element_type=jnp.float32)
        * score_scale
    )
    new_max = jnp.max(scores, axis=2)
    weights = jnp.exp(scores - new_max[:, :, None])
    shrink = jnp.exp(running_max - new_max)
    denominator = denominator * shrink + jnp.sum(weights, axis=2)
    weighted = weighted * shrink[:, :, None] + jnp.einsum(
        "qhk,khd->qhd",
        weights.astype(jnp.bfloat16),
        value_heads,
        preferred_element_type=jnp.float32,
    )
    return (new_max, denominator, weighted)


def initial_state(row_count, head_count):
    return (
        jnp.full((row_count, head_count), -jnp.inf, jnp.float32),
        jnp.zeros((row_count, head_count), jnp.float32),
        jnp.zeros((row_count, head_count, HEAD), jnp.float32),
    )


def on_device(query, keys, values, out_weight, out_gain):
    grouped_q, grouped_k, grouped_v = (
        lax.all_to_all(query, "uly", split_axis=1, concat_axis=0, tiled=True),
        lax.all_to_all(keys, "uly", split_axis=1, concat_axis=0, tiled=True),
        lax.all_to_all(values, "uly", split_axis=1, concat_axis=0, tiled=True),
    )
    row_count = grouped_q.shape[0]
    features = grouped_q.shape[1]
    local_heads = features // HEAD
    query_heads = grouped_q.reshape(row_count, local_heads, HEAD)
    half_heads = local_heads // 2
    half_width = half_heads * HEAD
    low_state = make_fold(
        query_heads[:, :half_heads],
        initial_state(row_count, half_heads),
        (
            lax.all_gather(grouped_k[:, :half_width], "blk", axis=0, tiled=True),
            lax.all_gather(grouped_v[:, :half_width], "blk", axis=0, tiled=True),
        ),
    )
    high_state = make_fold(
        query_heads[:, half_heads:],
        initial_state(row_count, local_heads - half_heads),
        (
            lax.all_gather(grouped_k[:, half_width:], "blk", axis=0, tiled=True),
            lax.all_gather(grouped_v[:, half_width:], "blk", axis=0, tiled=True),
        ),
    )
    denominator = jnp.concatenate([low_state[1], high_state[1]], axis=1)
    weighted = jnp.concatenate([low_state[2], high_state[2]], axis=1)
    attended = (
        (weighted / denominator[:, :, None]).reshape(row_count, features).astype(jnp.bfloat16)
    )
    partial_value = jnp.dot(
        attended,
        lax.all_gather(out_weight, "blk", axis=1, tiled=True),
        preferred_element_type=jnp.float32,
    )
    summed = lax.psum_scatter(
        partial_value.astype(jnp.bfloat16), "uly", scatter_dimension=0, tiled=True
    ).astype(jnp.float32)
    return (out_gain * summed).astype(jnp.bfloat16)


def attend_kernel(
    nb, nu,
    q_hbm, k_hbm, v_hbm, w_hbm, gain_hbm, out_ref,
    qkv_ref, gain_ref, stage, got, far, w_ref,
    att, acc, part_f32, part_send, part_got, final_send,
    in_sem, w_in, w_sent, w_came, a_sent, a_came, k_sent, k_came, up_sem,
    b_sent, b_came, b_last, passed, r_sent, r_came, f_sent, f_came,
):
    nx = nu // 2
    m = nb * nx
    rows, width = q_hbm.shape
    pairs = stage.shape[1]
    last = pairs - 1
    depth = w_hbm.shape[0]
    block = nx * rows
    mine_rows = nb * block
    side = nb // 2
    scale = math.log2(math.e) / math.sqrt(HEAD)
    me_b, me_u = lax.axis_index("blk"), lax.axis_index("uly")
    me_x, me_c = me_u // 2, lax.rem(me_u, 2)
    me = me_b * nx + me_x
    my_side = me_b // side
    gate_here = (side - 1) + my_side
    gate_there = side - my_side
    is_gate = me_b == gate_here
    far_side = (1 - my_side) * side

    def turn_of(b, e):
        upward = b // side
        return upward * e + (1 - upward) * (nb - 1 - e)

    def there(b, x):
        return dict(device_id={"blk": b, "uly": 2 * x + me_c}, device_id_type=MESH)

    partner = dict(device_id={"blk": me_b, "uly": 2 * me_x + 1 - me_c}, device_id_type=MESH)

    def await_bytes(ref, sem):
        pltpu.make_async_copy(ref, ref, sem).wait()

    def when(condition, action):
        pl.when(condition)(action)

    barrier = pltpu.get_barrier_semaphore()
    pl.semaphore_signal(barrier, inc=1, **partner)
    for d in range(1, nx):
        pl.semaphore_signal(barrier, inc=1, **there(me_b, lax.rem(me_x + d, nx)))
    for b in range(1, nb):

        @pl.when(b > me_b)
        def _():
            for x in range(nx):
                pl.semaphore_signal(barrier, inc=1, **there(b, x))

    for s, ref in enumerate((q_hbm, k_hbm, v_hbm)):
        pltpu.make_async_copy(ref, qkv_ref.at[s], in_sem).start()
    w_mine = w_ref.at[pl.ds(pl.multiple_of(me_c * depth, depth), depth)]
    with jax.named_scope("load"):
        await_bytes(qkv_ref, in_sem)
    w_load = pltpu.make_async_copy(w_hbm, w_mine, w_in)
    gain_load = pltpu.make_async_copy(gain_hbm, gain_ref, in_sem)
    w_load.start()
    gain_load.start()

    for b in range(nb):
        for x in range(nx):
            for p in range(pairs):
                at = ((x * nb + b) * pairs + p) * LANES
                for s in range(3):
                    stage[b * nx + x, p, s] = qkv_ref[s, :, pl.ds(at, LANES)]
    for p in range(pairs):
        for s in range(3):
            got[p, s, me] = stage[me, p, s]

    with jax.named_scope("barrier"):
        pl.semaphore_wait(barrier, me_b * nx + nx)
    for b in range(nb - 1):

        @pl.when(b < me_b)
        def _():
            for x in range(nx):
                pl.semaphore_signal(up_sem.at[me_b - 1], inc=1, **there(b, x))

    def ship(p, b, x):
        pltpu.make_async_remote_copy(
            src_ref=stage.at[b * nx + x, p], dst_ref=got.at[p, :, me],
            send_sem=a_sent, recv_sem=a_came.at[p], **there(b, x)).start()

    def ship_level(p, b):
        for d in range(nx - 1, -1, -1):
            ship(p, b, lax.rem(me_x + d, nx))

    def ship_beside(p):
        for d in range(1, nx):
            ship(p, me_b, lax.rem(me_x + d, nx))

    for p in range(pairs):
        for b in range(nb - 1):
            when(b < me_b, lambda: ship_level(p, b))
        ship_beside(p)

    w_swap = pltpu.make_async_remote_copy(
        src_ref=w_mine, dst_ref=w_mine, send_sem=w_sent, recv_sem=w_came, **partner)
    w_load.wait()
    gain_load.wait()
    w_swap.start()

    for b in range(1, nb):

        @pl.when(b > me_b)
        def _():
            with jax.named_scope(f"up{b}"):
                pl.semaphore_wait(up_sem.at[b - 1], nx)
            for p in range(min(2, pairs)):
                ship_level(p, b)
    for p in range(2, pairs):
        for b in range(nb - 1, 0, -1):
            when(b > me_b, lambda: ship_level(p, b))

    def swap(p):
        return pltpu.make_async_remote_copy(
            src_ref=got.at[p, pl.ds(1, 2)], dst_ref=far.at[p],
            send_sem=k_sent, recv_sem=k_came.at[p], **partner)

    def against(a, b):
        return lax.dot_general(a, b, (((1,), (1,)), ((), ())), preferred_element_type=jnp.float32)

    low = lax.broadcasted_iota(jnp.int32, (mine_rows, LANES), 1) < HEAD

    def target(d):
        return gate_there if d == 0 else my_side * side + lax.rem(me_b + d, side)

    def slot_of(origin, b):
        return origin - (origin > b)

    def spread(p, d, e):
        t = turn_of(target(d), e)
        whole = p < last
        piece = att.at[p, me_b] if whole else att.at[p, me_b, t]
        sem = b_came.at[p, me_b] if whole else b_last.at[me_b, t]
        pltpu.make_async_remote_copy(
            src_ref=piece, dst_ref=piece, send_sem=b_sent, recv_sem=sem,
            **there(target(d), me_x)).start()

    def spread_in(p, b, t):
        if p < last:
            await_bytes(att.at[p, b], b_came.at[p, b])
        else:
            await_bytes(att.at[p, b, t], b_last.at[b, t])

    def pass_on(p, d, b, t):
        whole = p < last
        piece = att.at[p, b] if whole else att.at[p, b, t]
        sem = b_came.at[p, b] if whole else b_last.at[b, t]
        pltpu.make_async_remote_copy(
            src_ref=piece, dst_ref=piece, send_sem=passed, recv_sem=sem,
            **there(target(d), me_x)).start()

    def spread_all(p):
        for e in range(nb if p == last else 1):
            for d in range(side):
                spread(p, d, e)

    def forward(p, t):
        for i in range(side):
            b = far_side + my_side * i + (1 - my_side) * (side - 1 - i)
            spread_in(p, b, t)

            @pl.when(is_gate)
            def _():
                for d in range(1, side):
                    pass_on(p, d, b, t)

    for p in range(pairs):
        with jax.named_scope(f"wA{p}"):
            await_bytes(got.at[p, :, pl.ds(0, m - 1)], a_came.at[p])
        swap(p).start()
        if p == last:
            for early in range(last):
                when(jnp.logical_not(is_gate), lambda: spread_all(early))
        q_all = jnp.concatenate([got[p, 0, i].astype(jnp.float32) for i in range(m)], axis=0)
        q_two = jnp.concatenate(
            [jnp.where(low, q_all, 0.0), jnp.where(low, 0.0, q_all)], axis=0).astype(jnp.bfloat16)
        with jax.named_scope(f"wK{p}"):
            await_bytes(far.at[p], k_came.at[p])
        k_all, v_all = (
            jnp.concatenate(
                [got[p, s, i].astype(jnp.float32) for i in range(m)]
                + [far[p, s - 1, i].astype(jnp.float32) for i in range(m)], axis=0
            ).astype(jnp.bfloat16)
            for s in (1, 2))
        scores = against(q_two, k_all)
        top = jnp.max(scores, axis=1, keepdims=True)
        weights = jnp.exp2((scores - top) * scale)
        total = jnp.sum(weights, axis=1, keepdims=True)
        both = jnp.dot(
            weights.astype(jnp.bfloat16), v_all, preferred_element_type=jnp.float32) / total
        joined = jnp.where(low, both[:mine_rows], both[mine_rows:]).astype(jnp.bfloat16)
        for t in range(nb):
            att[p, me_b, t] = joined[t * block:(t + 1) * block]
        with jax.named_scope(f"sB{p}"):
            if p == last:
                spread_all(p)
            else:
                when(is_gate, lambda: spread_all(p))

    def settle(p, t):
        forward(p, t)
        for d in range(1, side):
            spread_in(p, target(d), t)

    def weight_of(p):
        return jnp.concatenate(
            [w_ref[pl.ds((b * pairs + p) * LANES, LANES)] for b in range(nb)], axis=0)

    with jax.named_scope("wW"):
        await_bytes(w_mine, w_came)
    for p in range(last):
        with jax.named_scope(f"wB{p}"):
            settle(p, 0)
        seen = jnp.concatenate(
            [att[p, b].reshape(mine_rows, LANES) for b in range(nb)], axis=1)
        part = jnp.dot(seen, weight_of(p), preferred_element_type=jnp.float32).reshape(acc.shape)
        if p == 0:
            acc[...] = part
        else:
            acc[...] += part

    def scatter(t, d):
        x = lax.rem(me_x + d, nx)
        pltpu.make_async_remote_copy(
            src_ref=part_send.at[t, x], dst_ref=part_got.at[t, me_x],
            send_sem=r_sent, recv_sem=r_came.at[t, d - 1], **there(me_b, x)).start()

    def reduce(e):
        t = turn_of(me_b, e)
        total = part_f32[t, me_x]
        for d in range(1, nx):
            x = lax.rem(me_x + nx - d, nx)
            with jax.named_scope(f"wR{e}"):
                await_bytes(part_got.at[t, x], r_came.at[t, d - 1])
            total += part_got[t, x].astype(jnp.float32)
        gated = (gain_ref[me_b] * total).astype(jnp.bfloat16)

        @pl.when(me_b == t)
        def _():
            out_ref[t] = gated

        @pl.when(me_b != t)
        def _():
            final_send[t] = gated
            pltpu.make_async_remote_copy(
                src_ref=final_send.at[t], dst_ref=out_ref.at[me_b],
                send_sem=f_sent, recv_sem=f_came, **there(t, me_x)).start()

    for e in range(nb):
        t = turn_of(me_b, e)
        with jax.named_scope(f"wBl{e}"):
            settle(last, t)
        seen = jnp.concatenate([att[last, b, t] for b in range(nb)], axis=1)
        part = jnp.dot(seen, weight_of(last), preferred_element_type=jnp.float32)
        if pairs > 1:
            part += acc[t]
        for x in range(nx):
            one = part[x * rows:(x + 1) * rows]
            part_f32[t, x] = one
            part_send[t, x] = one.astype(jnp.bfloat16)
        for d in range(1, nx):
            scatter(t, d)
        if e >= 2:
            reduce(e - 2)
    for e in range(nb - 2, nb):
        reduce(e)

    with jax.named_scope("wF"):
        await_bytes(out_ref.at[pl.ds(0, nb - 1)], f_came)

    with jax.named_scope("drain"):
        w_swap.wait_send()
        await_bytes(stage.at[pl.ds(0, m - 1)], a_sent)
        await_bytes(far, k_sent)
        await_bytes(att.at[:, pl.ds(0, side)], b_sent)

        @pl.when(is_gate)
        def _():
            await_bytes(att.at[:, pl.ds(0, side * (side - 1))], passed)

        await_bytes(part_send.at[:, pl.ds(0, nx - 1)], r_sent)
        await_bytes(final_send.at[pl.ds(0, nb - 1)], f_sent)


def fused(nb, nu, query, keys, values, out_weight, out_gain):
    nx = nu // 2
    m = nb * nx
    rows, width = query.shape
    pairs = width // LANES // m
    depth, columns = out_weight.shape
    bf16, f32 = jnp.bfloat16, jnp.float32
    vmem, dma = pltpu.VMEM, pltpu.SemaphoreType.DMA
    in_hbm = pl.BlockSpec(memory_space=pltpu.HBM)
    block = nx * rows
    gathered = pl.pallas_call(
        functools.partial(attend_kernel, nb, nu),
        out_shape=vmem((nb, rows, columns), bf16),
        in_specs=[in_hbm] * 5,
        out_specs=pl.BlockSpec(memory_space=pltpu.VMEM),
        scratch_shapes=[
            vmem((3, rows, width), bf16),
            vmem((nb, 1, columns), f32),
            vmem((m, pairs, 3, rows, LANES), bf16),
            vmem((pairs, 3, m, rows, LANES), bf16),
            vmem((pairs, 2, m, rows, LANES), bf16),
            vmem((2 * depth, columns), bf16),
            vmem((pairs, nb, nb, block, LANES), bf16),
            vmem((nb, block, columns), f32),
            vmem((nb, nx, rows, columns), f32),
            vmem((nb, nx, rows, columns), bf16),
            vmem((nb, nx, rows, columns), bf16),
            vmem((nb, rows, columns), bf16),
            dma, dma, dma, dma, dma, dma((pairs,)), dma, dma((pairs,)),
            pltpu.SemaphoreType.REGULAR((nb - 1,)),
            dma, dma((pairs, nb)), dma((nb, nb)), dma, dma, dma((nb, nx - 1)), dma, dma,
        ],
        compiler_params=pltpu.CompilerParams(
            collective_id=0, has_side_effects=True),
    )(query, keys, values, out_weight, out_gain.reshape(nb, 1, columns))
    return gathered.transpose(1, 0, 2).reshape(rows, width)


def on_any(nb, nu, query, keys, values, out_weight, out_gain):
    rows, width = query.shape
    suits = (
        nu % 2 == 0 and nu > 2 and nb % 2 == 0 and width % (LANES * nb * nu // 2) == 0
        and rows % 8 == 0 and (nu // 2 * rows) % 16 == 0 and (width // nb) % LANES == 0
    )
    plan = functools.partial(fused, nb, nu) if suits else on_device
    return plan(query, keys, values, out_weight, out_gain)


def solution(mesh):
    in_specs = (
        P(("group", "blk", "uly"), None),
        P(("group", "blk", "uly"), None),
        P(("group", "blk", "uly"), None),
        P("uly", "blk"),
        P(),
    )
    out_specs = P(("group", "blk", "uly"), None)
    body = functools.partial(on_any, mesh.shape["blk"], mesh.shape["uly"])
    return jax.shard_map(
        body, mesh=mesh, in_specs=in_specs, out_specs=out_specs, check_vma=False
    )
```

time: 40.9 us -> 37.5 us (0.917)
  Pallas kernels: 39.1 us -> 36.7 us
  local copies, waits for them, and re-layouts: 1.58 us -> 0.67 us
    pallas_call x1, Pallas kernels: 39.1 us -> 36.7 us  [fused(): pl.pallas_call(functools.partial(attend_kernel, nb, nu), out_shape=vmem((...]
    reshape x1, local copies, waits for them, and re-layouts: 1.58 us -> 0.67 us  [fused(): return gathered.transpose(1, 0, 2).reshape(rows, width)]
where the time goes in v2:
time: 37.5 us; the launch traced here: 37.4 us
  Pallas kernels  36.7 us (98%)
  local copies, waits for them, and re-layouts  0.67 us (2%)
    pallas_call x1, Pallas kernels, fused(): pl.pallas_call(functools.partial(attend_kernel, nb, nu), out_shape=vmem((...  36.7 us

profile of v2, /device:TPU:0, one launch (start us, length us, event | category | flops | bytes accessed | tf_op | source)
XLA Modules:
  0.0 37.4 jit_solution(8557517053278623965)
XLA Ops:
  0.0 36.7 %shard_map.55 = bf16[4,24,768]{2,1,0:T(8,128)(2,1)S(1)} custom-call(bf16[24,3072]{1,0:T(8,128)(2,1)} %q_hbm.1, bf16[24,3072]{1,0:T(8,128)(2,1)} %k_hbm.1, bf16[24,3072]{1,0:T(8,128)(2,1)} %v_hbm.1, bf16[768,768]{1,0:T(8,128)(2,1)} %w_hbm.1, f32[4,1,768]{2,1,0:T(1,128)} %bitcast.5), custom_call_target="tpu_custom_call" | custom-call | tf_op jit(solution)/shard_map/pallas_call | solution.py:392
  36.7 0.7 %copy.7 = bf16[4,3,8,768]{3,2,0,1:T(8,128)(2,1)} copy(bf16[4,3,8,768]{3,2,1,0:T(8,128)(2,1)S(1)} %bitcast.4) | data formatting | bytes 294912 | tf_op jit(solution)/shard_map/reshape | solution.py:417

commit v3 on v2

--- a/solution.py
+++ b/solution.py
@@ -114,6 +114,7 @@
     gate_here = (side - 1) + my_side
     gate_there = side - my_side
     is_gate = me_b == gate_here
+    held = (me_b < side) & jnp.logical_not(is_gate)
     far_side = (1 - my_side) * side
 
     def turn_of(b, e):
@@ -145,6 +146,15 @@
     for s, ref in enumerate((q_hbm, k_hbm, v_hbm)):
         pltpu.make_async_copy(ref, qkv_ref.at[s], in_sem).start()
     w_mine = w_ref.at[pl.ds(pl.multiple_of(me_c * depth, depth), depth)]
+    with jax.named_scope("barrier"):
+        pl.semaphore_wait(barrier, me_b * nx + nx)
+    for b in range(nb - 1):
+
+        @pl.when(b < me_b)
+        def _():
+            for x in range(nx):
+                pl.semaphore_signal(up_sem.at[me_b - 1], inc=1, **there(b, x))
+
     with jax.named_scope("load"):
         await_bytes(qkv_ref, in_sem)
     w_load = pltpu.make_async_copy(w_hbm, w_mine, w_in)
@@ -162,14 +172,6 @@
         for s in range(3):
             got[p, s, me] = stage[me, p, s]
 
-    with jax.named_scope("barrier"):
-        pl.semaphore_wait(barrier, me_b * nx + nx)
-    for b in range(nb - 1):
-
-        @pl.when(b < me_b)
-        def _():
-            for x in range(nx):
-                pl.semaphore_signal(up_sem.at[me_b - 1], inc=1, **there(b, x))
 
     def ship(p, b, x):
         pltpu.make_async_remote_copy(
@@ -201,11 +203,11 @@
         def _():
             with jax.named_scope(f"up{b}"):
                 pl.semaphore_wait(up_sem.at[b - 1], nx)
-            for p in range(min(2, pairs)):
+            for p in range(min(1, pairs)):
                 ship_level(p, b)
-    for p in range(2, pairs):
+    for p in range(1, pairs):
         for b in range(nb - 1, 0, -1):
-            when(b > me_b, lambda: ship_level(p, b))
+            when((b > me_b) & (me_b > 0), lambda: ship_level(p, b))
 
     def swap(p):
         return pltpu.make_async_remote_copy(
@@ -246,28 +248,32 @@
             src_ref=piece, dst_ref=piece, send_sem=passed, recv_sem=sem,
             **there(target(d), me_x)).start()
 
-    def spread_all(p):
+    def spread_near(p):
         for e in range(nb if p == last else 1):
-            for d in range(side):
+            for d in range(1, side):
                 spread(p, d, e)
 
     def forward(p, t):
-        for i in range(side):
-            b = far_side + my_side * i + (1 - my_side) * (side - 1 - i)
-            spread_in(p, b, t)
-
-            @pl.when(is_gate)
-            def _():
+        @pl.when(is_gate)
+        def _():
+            for i in range(side):
+                b = far_side + my_side * i + (1 - my_side) * (side - 1 - i)
+                spread_in(p, b, t)
                 for d in range(1, side):
                     pass_on(p, d, b, t)
 
     for p in range(pairs):
         with jax.named_scope(f"wA{p}"):
             await_bytes(got.at[p, :, pl.ds(0, m - 1)], a_came.at[p])
+        if p == 0:
+            for later in range(1, pairs):
+                for b in range(nb - 1, 0, -1):
+                    when((b > me_b) & (me_b == 0), lambda: ship_level(later, b))
         swap(p).start()
         if p == last:
             for early in range(last):
-                when(jnp.logical_not(is_gate), lambda: spread_all(early))
+                when(held, lambda: spread(early, 0, 0))
+            forward(0, 0)
         q_all = jnp.concatenate([got[p, 0, i].astype(jnp.float32) for i in range(m)], axis=0)
         q_two = jnp.concatenate(
             [jnp.where(low, q_all, 0.0), jnp.where(low, 0.0, q_all)], axis=0).astype(jnp.bfloat16)
@@ -289,13 +295,26 @@
         for t in range(nb):
             att[p, me_b, t] = joined[t * block:(t + 1) * block]
         with jax.named_scope(f"sB{p}"):
-            if p == last:
-                spread_all(p)
+            if p < last:
+                when(jnp.logical_not(held), lambda: spread(p, 0, 0))
+                when(is_gate, lambda: spread_near(p))
             else:
-                when(is_gate, lambda: spread_all(p))
+                for e in range(nb):
+                    spread(p, 0, e)
+                for early in range(1 if True else 0, last):
+                    forward(early, 0)
+                for early in range(last):
+                    when(jnp.logical_not(is_gate), lambda: spread_near(early))
+                spread_near(p)
 
     def settle(p, t):
-        forward(p, t)
+        @pl.when(jnp.logical_not(is_gate))
+        def _():
+            for i in range(side):
+                spread_in(p, far_side + i, t)
+
+        if p == last:
+            forward(p, t)
         for d in range(1, side):
             spread_in(p, target(d), t)
 
@@ -357,9 +376,9 @@
             part_send[t, x] = one.astype(jnp.bfloat16)
         for d in range(1, nx):
             scatter(t, d)
-        if e >= 2:
-            reduce(e - 2)
-    for e in range(nb - 2, nb):
+        if e >= 4:
+            reduce(e - 4)
+    for e in range(nb - 4, nb):
         reduce(e)
 
     with jax.named_scope("wF"):

time: 37.5 us -> 35.8 us (0.955)
  Pallas kernels: 36.7 us -> 35 us
    pallas_call x1, Pallas kernels: 36.7 us -> 35 us  [fused(): pl.pallas_call(functools.partial(attend_kernel, nb, nu), out_shape=vmem((...]
where the time goes in v3:
time: 35.8 us; the launch traced here: 35.7 us
  Pallas kernels  35 us (98%)
  local copies, waits for them, and re-layouts  0.67 us (2%)
    pallas_call x1, Pallas kernels, fused(): pl.pallas_call(functools.partial(attend_kernel, nb, nu), out_shape=vmem((...  35 us

profile of v3, /device:TPU:0, one launch (start us, length us, event | category | flops | bytes accessed | tf_op | source)
XLA Modules:
  0.0 35.7 jit_solution(2270534432665750739)
XLA Ops:
  0.0 35.0 %shard_map.55 = bf16[4,24,768]{2,1,0:T(8,128)(2,1)S(1)} custom-call(bf16[24,3072]{1,0:T(8,128)(2,1)} %q_hbm.1, bf16[24,3072]{1,0:T(8,128)(2,1)} %k_hbm.1, bf16[24,3072]{1,0:T(8,128)(2,1)} %v_hbm.1, bf16[768,768]{1,0:T(8,128)(2,1)} %w_hbm.1, f32[4,1,768]{2,1,0:T(1,128)} %bitcast.5), custom_call_target="tpu_custom_call" | custom-call | tf_op jit(solution)/shard_map/pallas_call | solution.py:411
  35.0 0.7 %copy.7 = bf16[4,3,8,768]{3,2,0,1:T(8,128)(2,1)} copy(bf16[4,3,8,768]{3,2,1,0:T(8,128)(2,1)S(1)} %bitcast.4) | data formatting | bytes 294912 | tf_op jit(solution)/shard_map/reshape | solution.py:436

commit v4 on v3

--- a/solution.py
+++ b/solution.py
@@ -114,7 +114,7 @@
     gate_here = (side - 1) + my_side
     gate_there = side - my_side
     is_gate = me_b == gate_here
-    held = (me_b < side) & jnp.logical_not(is_gate)
+    held = me_b < 0
     far_side = (1 - my_side) * side
 
     def turn_of(b, e):
@@ -203,11 +203,10 @@
         def _():
             with jax.named_scope(f"up{b}"):
                 pl.semaphore_wait(up_sem.at[b - 1], nx)
-            for p in range(min(1, pairs)):
-                ship_level(p, b)
+            ship_level(0, b)
     for p in range(1, pairs):
         for b in range(nb - 1, 0, -1):
-            when((b > me_b) & (me_b > 0), lambda: ship_level(p, b))
+            when((b > me_b) & ((me_b > 0) | (b == 1)), lambda: ship_level(p, b))
 
     def swap(p):
         return pltpu.make_async_remote_copy(
@@ -222,63 +221,73 @@
     def target(d):
         return gate_there if d == 0 else my_side * side + lax.rem(me_b + d, side)
 
-    def slot_of(origin, b):
-        return origin - (origin > b)
-
-    def spread(p, d, e):
-        t = turn_of(target(d), e)
-        whole = p < last
-        piece = att.at[p, me_b] if whole else att.at[p, me_b, t]
-        sem = b_came.at[p, me_b] if whole else b_last.at[me_b, t]
+    def came(p, b, t):
+        return b_came.at[p, b] if t is None else b_last.at[b, t]
+
+    def piece(p, b, t):
+        return att.at[p, b] if t is None else att.at[p, b, t]
+
+    def push(p, d, b, t, sent, sem):
         pltpu.make_async_remote_copy(
-            src_ref=piece, dst_ref=piece, send_sem=b_sent, recv_sem=sem,
+            src_ref=piece(p, b, t), dst_ref=piece(p, b, t), send_sem=sent, recv_sem=sem,
             **there(target(d), me_x)).start()
 
-    def spread_in(p, b, t):
+    def spread(p, d):
         if p < last:
-            await_bytes(att.at[p, b], b_came.at[p, b])
+            push(p, d, me_b, None, b_sent, came(p, me_b, None))
         else:
-            await_bytes(att.at[p, b, t], b_last.at[b, t])
-
-    def pass_on(p, d, b, t):
-        whole = p < last
-        piece = att.at[p, b] if whole else att.at[p, b, t]
-        sem = b_came.at[p, b] if whole else b_last.at[b, t]
-        pltpu.make_async_remote_copy(
-            src_ref=piece, dst_ref=piece, send_sem=passed, recv_sem=sem,
-            **there(target(d), me_x)).start()
+            for e in range(nb):
+                t = turn_of(target(d), e)
+                push(p, d, me_b, t, b_sent, came(p, me_b, t))
 
     def spread_near(p):
-        for e in range(nb if p == last else 1):
-            for d in range(1, side):
-                spread(p, d, e)
-
-    def forward(p, t):
-        @pl.when(is_gate)
-        def _():
-            for i in range(side):
-                b = far_side + my_side * i + (1 - my_side) * (side - 1 - i)
-                spread_in(p, b, t)
-                for d in range(1, side):
-                    pass_on(p, d, b, t)
+        for d in range(1, side):
+            spread(p, d)
+
+    def far_of(i):
+        return far_side + my_side * i + (1 - my_side) * (side - 1 - i)
+
+    def near_of(d):
+        return my_side * side + lax.rem(me_b + d, side)
+
+    upper = my_side == 1
+    late_core = (me_b < side) & (me_c == 1)
+
+    def forward(p, turns, whose, fresh=True, only=True):
+        @pl.when(is_gate & only)
+        def _():
+            for e in turns:
+                t = turn_of(me_b, e)
+                for i in whose:
+                    b = far_of(i)
+                    if p == last:
+                        await_bytes(att.at[p, b, t], b_last.at[b, t])
+                    elif fresh and e == turns[0]:
+                        await_bytes(att.at[p, b], b_came.at[p, b])
+                    for d in range(1, side):
+                        push(p, d, b, t, passed, came(p, b, t))
+
+    every = list(range(side))
+    head, tail = range(nb - 1), range(nb - 1, nb)
 
     for p in range(pairs):
         with jax.named_scope(f"wA{p}"):
             await_bytes(got.at[p, :, pl.ds(0, m - 1)], a_came.at[p])
         if p == 0:
-            for later in range(1, pairs):
-                for b in range(nb - 1, 0, -1):
-                    when((b > me_b) & (me_b == 0), lambda: ship_level(later, b))
+            for later in range(1, min(2, pairs)):
+                for b in range(nb - 1, 1, -1):
+                    when(me_b == 0, lambda: ship_level(later, b))
         swap(p).start()
         if p == last:
             for early in range(last):
-                when(held, lambda: spread(early, 0, 0))
-            forward(0, 0)
+                when(held, lambda: spread(early, 0))
         q_all = jnp.concatenate([got[p, 0, i].astype(jnp.float32) for i in range(m)], axis=0)
         q_two = jnp.concatenate(
             [jnp.where(low, q_all, 0.0), jnp.where(low, 0.0, q_all)], axis=0).astype(jnp.bfloat16)
         with jax.named_scope(f"wK{p}"):
             await_bytes(far.at[p], k_came.at[p])
+        if p == last and last > 0:
+            when(late_core, lambda: spread(last - 1, 0))
         k_all, v_all = (
             jnp.concatenate(
                 [got[p, s, i].astype(jnp.float32) for i in range(m)]
@@ -296,44 +305,54 @@
             att[p, me_b, t] = joined[t * block:(t + 1) * block]
         with jax.named_scope(f"sB{p}"):
             if p < last:
-                when(jnp.logical_not(held), lambda: spread(p, 0, 0))
+                when(jnp.logical_not(held | (late_core & (p == last - 1))), lambda: spread(p, 0))
+                if p == 0:
+                    for later in range(2, pairs):
+                        for b in range(nb - 1, 1, -1):
+                            when(me_b == 0, lambda: ship_level(later, b))
                 when(is_gate, lambda: spread_near(p))
+                if p == last - 1:
+                    for early, i in ((0, 0),):
+                        with jax.named_scope(f"fa{early}{i}"):
+                            forward(early, head, [i], only=upper)
             else:
-                for e in range(nb):
-                    spread(p, 0, e)
-                for early in range(1 if True else 0, last):
-                    forward(early, 0)
+                spread(p, 0)
+                for early in range(last):
+                    with jax.named_scope(f"fw{early}"):
+                        for i in every:
+                            if (early, i) in ((0, 0),):
+                                forward(early, head, [i], only=jnp.logical_not(upper))
+                            else:
+                                forward(early, head, [i])
                 for early in range(last):
                     when(jnp.logical_not(is_gate), lambda: spread_near(early))
                 spread_near(p)
-
-    def settle(p, t):
-        @pl.when(jnp.logical_not(is_gate))
-        def _():
-            for i in range(side):
-                spread_in(p, far_side + i, t)
-
-        if p == last:
-            forward(p, t)
-        for d in range(1, side):
-            spread_in(p, target(d), t)
-
-    def weight_of(p):
-        return jnp.concatenate(
-            [w_ref[pl.ds((b * pairs + p) * LANES, LANES)] for b in range(nb)], axis=0)
+                with jax.named_scope(f"fwl"):
+                    forward(last, head, every)
+                for early in range(last):
+                    forward(early, tail, every, fresh=False)
+                with jax.named_scope(f"fwm"):
+                    forward(last, tail, every)
+
+    def weight_of(p, b):
+        at = pl.multiple_of((b * pairs + p) * LANES, LANES)
+        return w_ref[pl.ds(at, LANES)]
+
+    beside = [near_of(d) for d in range(side)]
+    across = [far_side + i for i in range(side)]
 
     with jax.named_scope("wW"):
         await_bytes(w_mine, w_came)
     for p in range(last):
-        with jax.named_scope(f"wB{p}"):
-            settle(p, 0)
-        seen = jnp.concatenate(
-            [att[p, b].reshape(mine_rows, LANES) for b in range(nb)], axis=1)
-        part = jnp.dot(seen, weight_of(p), preferred_element_type=jnp.float32).reshape(acc.shape)
-        if p == 0:
-            acc[...] = part
-        else:
-            acc[...] += part
+        for d in range(1, side):
+            with jax.named_scope(f"wB{p}"):
+                await_bytes(att.at[p, beside[d]], b_came.at[p, beside[d]])
+    if last:
+        early = [(p, b) for p in range(last) for b in beside]
+        seen = jnp.concatenate([att[p, b].reshape(mine_rows, LANES) for p, b in early], axis=1)
+        weight = jnp.concatenate([weight_of(p, b) for p, b in early], axis=0)
+        acc[...] = jnp.dot(seen, weight, preferred_element_type=jnp.float32).reshape(acc.shape)
+    late = [(p, b) for p in range(pairs) for b in across] + [(last, b) for b in beside]
 
     def scatter(t, d):
         x = lax.rem(me_x + d, nx)
@@ -365,10 +384,17 @@
     for e in range(nb):
         t = turn_of(me_b, e)
         with jax.named_scope(f"wBl{e}"):
-            settle(last, t)
-        seen = jnp.concatenate([att[last, b, t] for b in range(nb)], axis=1)
-        part = jnp.dot(seen, weight_of(last), preferred_element_type=jnp.float32)
-        if pairs > 1:
+            @pl.when(jnp.logical_not(is_gate))
+            def _():
+                for b in across:
+                    await_bytes(att.at[:, b, t], b_last.at[b, t])
+
+            for d in range(1, side):
+                await_bytes(att.at[last, beside[d], t], b_last.at[beside[d], t])
+        seen = jnp.concatenate([att[p, b, t] for p, b in late], axis=1)
+        weight = jnp.concatenate([weight_of(p, b) for p, b in late], axis=0)
+        part = jnp.dot(seen, weight, preferred_element_type=jnp.float32)
+        if last:
             part += acc[t]
         for x in range(nx):
             one = part[x * rows:(x + 1) * rows]

time: 35.8 us -> 34.3 us (0.958)
  Pallas kernels: 35 us -> 33.5 us
    pallas_call x1, Pallas kernels: 35 us -> 33.5 us  [fused(): pl.pallas_call(functools.partial(attend_kernel, nb, nu), out_shape=vmem((...]
where the time goes in v4:
time: 34.3 us; the launch traced here: 34.2 us
  Pallas kernels  33.5 us (98%)
  local copies, waits for them, and re-layouts  0.67 us (2%)
    pallas_call x1, Pallas kernels, fused(): pl.pallas_call(functools.partial(attend_kernel, nb, nu), out_shape=vmem((...  33.5 us

profile of v4, /device:TPU:0, one launch (start us, length us, event | category | flops | bytes accessed | tf_op | source)
XLA Modules:
  0.0 34.2 jit_solution(16502442871863454050)
XLA Ops:
  0.0 33.5 %shard_map.55 = bf16[4,24,768]{2,1,0:T(8,128)(2,1)S(1)} custom-call(bf16[24,3072]{1,0:T(8,128)(2,1)} %q_hbm.1, bf16[24,3072]{1,0:T(8,128)(2,1)} %k_hbm.1, bf16[24,3072]{1,0:T(8,128)(2,1)} %v_hbm.1, bf16[768,768]{1,0:T(8,128)(2,1)} %w_hbm.1, f32[4,1,768]{2,1,0:T(1,128)} %bitcast.5), custom_call_target="tpu_custom_call" | custom-call | tf_op jit(solution)/shard_map/pallas_call | solution.py:437
  33.5 0.7 %copy.7 = bf16[4,3,8,768]{3,2,0,1:T(8,128)(2,1)} copy(bf16[4,3,8,768]{3,2,1,0:T(8,128)(2,1)S(1)} %bitcast.4) | data formatting | bytes 294912 | tf_op jit(solution)/shard_map/reshape | solution.py:462

commit v5 on v4

--- a/solution.py
+++ b/solution.py
@@ -120,6 +120,12 @@
     def turn_of(b, e):
         upward = b // side
         return upward * e + (1 - upward) * (nb - 1 - e)
+
+    def order_here(e):
+        if e == nb - 1:
+            return me_b
+        down = nb - 1 - e
+        return my_side * (e + (e >= me_b)) + (1 - my_side) * (down - (down <= me_b))
 
     def there(b, x):
         return dict(device_id={"blk": b, "uly": 2 * x + me_c}, device_id_type=MESH)
@@ -361,7 +367,7 @@
             send_sem=r_sent, recv_sem=r_came.at[t, d - 1], **there(me_b, x)).start()
 
     def reduce(e):
-        t = turn_of(me_b, e)
+        t = order_here(e)
         total = part_f32[t, me_x]
         for d in range(1, nx):
             x = lax.rem(me_x + nx - d, nx)
@@ -382,7 +388,7 @@
                 send_sem=f_sent, recv_sem=f_came, **there(t, me_x)).start()
 
     for e in range(nb):
-        t = turn_of(me_b, e)
+        t = order_here(e)
         with jax.named_scope(f"wBl{e}"):
             @pl.when(jnp.logical_not(is_gate))
             def _():

time: 34.3 us -> 33.6 us (0.980)
  Pallas kernels: 33.5 us -> 32.8 us
    pallas_call x1, Pallas kernels: 33.5 us -> 32.8 us  [fused(): pl.pallas_call(functools.partial(attend_kernel, nb, nu), out_shape=vmem((...]
where the time goes in v5:
time: 33.6 us; the launch traced here: 33.4 us
  Pallas kernels  32.8 us (98%)
  local copies, waits for them, and re-layouts  0.67 us (2%)
    pallas_call x1, Pallas kernels, fused(): pl.pallas_call(functools.partial(attend_kernel, nb, nu), out_shape=vmem((...  32.8 us
    reshape x1, local copies, waits for them, and re-layouts, fused(): return gathered.transpose(1, 0, 2).reshape(rows, width)  0.67 us

profile of v5, /device:TPU:0, one launch (start us, length us, event | category | flops | bytes accessed | tf_op | source)
XLA Modules:
  0.0 33.4 jit_solution(8879070200949786251)
XLA Ops:
  0.0 32.8 %shard_map.55 = bf16[4,24,768]{2,1,0:T(8,128)(2,1)S(1)} custom-call(bf16[24,3072]{1,0:T(8,128)(2,1)} %q_hbm.1, bf16[24,3072]{1,0:T(8,128)(2,1)} %k_hbm.1, bf16[24,3072]{1,0:T(8,128)(2,1)} %v_hbm.1, bf16[768,768]{1,0:T(8,128)(2,1)} %w_hbm.1, f32[4,1,768]{2,1,0:T(1,128)} %bitcast.5), custom_call_target="tpu_custom_call" | custom-call | tf_op jit(solution)/shard_map/pallas_call | solution.py:443
  32.8 0.7 %copy.7 = bf16[4,3,8,768]{3,2,0,1:T(8,128)(2,1)} copy(bf16[4,3,8,768]{3,2,1,0:T(8,128)(2,1)S(1)} %bitcast.4) | data formatting | bytes 294912 | tf_op jit(solution)/shard_map/reshape | solution.py:468

commit v6 on v5

--- a/solution.py
+++ b/solution.py
@@ -93,9 +93,9 @@
     nb, nu,
     q_hbm, k_hbm, v_hbm, w_hbm, gain_hbm, out_ref,
     qkv_ref, gain_ref, stage, got, far, w_ref,
-    att, acc, part_f32, part_send, part_got, final_send,
+    att, acc, part_f32, part_send, part_got, final_send, direct_got,
     in_sem, w_in, w_sent, w_came, a_sent, a_came, k_sent, k_came, up_sem,
-    b_sent, b_came, b_last, passed, r_sent, r_came, f_sent, f_came,
+    b_sent, b_came, b_last, passed, r_sent, r_came, f_sent, f_came, d_sent, d_came,
 ):
     nx = nu // 2
     m = nb * nx
@@ -118,14 +118,16 @@
     far_side = (1 - my_side) * side
 
     def turn_of(b, e):
+        low = nb - 1 if e == nb - 1 else (e + 1) % (nb - 1)
         upward = b // side
-        return upward * e + (1 - upward) * (nb - 1 - e)
+        return upward * e + (1 - upward) * low
+
+    is_end = ((me_b == 0) | (me_b == nb - 1)) & (nb > 2)
+    opposite = nb - 1 - me_b
 
     def order_here(e):
-        if e == nb - 1:
-            return me_b
-        down = nb - 1 - e
-        return my_side * (e + (e >= me_b)) + (1 - my_side) * (down - (down <= me_b))
+        own_last = me_b if e == nb - 1 else e + (e >= me_b)
+        return is_gate * own_last + (1 - is_gate) * turn_of(me_b, e)
 
     def there(b, x):
         return dict(device_id={"blk": b, "uly": 2 * x + me_c}, device_id_type=MESH)
@@ -275,6 +277,25 @@
 
     every = list(range(side))
     head, tail = range(nb - 1), range(nb - 1, nb)
+
+    beside = [near_of(d) for d in range(side)]
+    across = [far_side + i for i in range(side)]
+
+    def weight_of(p, b):
+        at = pl.multiple_of((b * pairs + p) * LANES, LANES)
+        return w_ref[pl.ds(at, LANES)]
+
+    def fill_early():
+        await_bytes(w_mine, w_came)
+        for p in range(last):
+            for d in range(1, side):
+                with jax.named_scope(f"wB{p}"):
+                    await_bytes(att.at[p, beside[d]], b_came.at[p, beside[d]])
+        if last:
+            early = [(p, b) for p in range(last) for b in beside]
+            seen = jnp.concatenate([att[p, b].reshape(mine_rows, LANES) for p, b in early], axis=1)
+            weight = jnp.concatenate([weight_of(p, b) for p, b in early], axis=0)
+            acc[...] = jnp.dot(seen, weight, preferred_element_type=jnp.float32).reshape(acc.shape)
 
     for p in range(pairs):
         with jax.named_scope(f"wA{p}"):
@@ -294,6 +315,7 @@
             await_bytes(far.at[p], k_came.at[p])
         if p == last and last > 0:
             when(late_core, lambda: spread(last - 1, 0))
+            when(jnp.logical_not(is_gate), lambda: spread_near(last - 1))
         k_all, v_all = (
             jnp.concatenate(
                 [got[p, s, i].astype(jnp.float32) for i in range(m)]
@@ -311,14 +333,16 @@
             att[p, me_b, t] = joined[t * block:(t + 1) * block]
         with jax.named_scope(f"sB{p}"):
             if p < last:
-                when(jnp.logical_not(held | (late_core & (p == last - 1))), lambda: spread(p, 0))
                 if p == 0:
                     for later in range(2, pairs):
                         for b in range(nb - 1, 1, -1):
                             when(me_b == 0, lambda: ship_level(later, b))
+                when(jnp.logical_not(held | (late_core & (p == last - 1))), lambda: spread(p, 0))
                 when(is_gate, lambda: spread_near(p))
                 if p == last - 1:
-                    for early, i in ((0, 0),):
+                    for early in range(p):
+                        when(jnp.logical_not(is_gate), lambda: spread_near(early))
+                    for early, i in ():
                         with jax.named_scope(f"fa{early}{i}"):
                             forward(early, head, [i], only=upper)
             else:
@@ -326,13 +350,12 @@
                 for early in range(last):
                     with jax.named_scope(f"fw{early}"):
                         for i in every:
-                            if (early, i) in ((0, 0),):
+                            if (early, i) in ():
                                 forward(early, head, [i], only=jnp.logical_not(upper))
                             else:
                                 forward(early, head, [i])
-                for early in range(last):
-                    when(jnp.logical_not(is_gate), lambda: spread_near(early))
                 spread_near(p)
+                fill_early()
                 with jax.named_scope(f"fwl"):
                     forward(last, head, every)
                 for early in range(last):
@@ -340,24 +363,6 @@
                 with jax.named_scope(f"fwm"):
                     forward(last, tail, every)
 
-    def weight_of(p, b):
-        at = pl.multiple_of((b * pairs + p) * LANES, LANES)
-        return w_ref[pl.ds(at, LANES)]
-
-    beside = [near_of(d) for d in range(side)]
-    across = [far_side + i for i in range(side)]
-
-    with jax.named_scope("wW"):
-        await_bytes(w_mine, w_came)
-    for p in range(last):
-        for d in range(1, side):
-            with jax.named_scope(f"wB{p}"):
-                await_bytes(att.at[p, beside[d]], b_came.at[p, beside[d]])
-    if last:
-        early = [(p, b) for p in range(last) for b in beside]
-        seen = jnp.concatenate([att[p, b].reshape(mine_rows, LANES) for p, b in early], axis=1)
-        weight = jnp.concatenate([weight_of(p, b) for p, b in early], axis=0)
-        acc[...] = jnp.dot(seen, weight, preferred_element_type=jnp.float32).reshape(acc.shape)
     late = [(p, b) for p in range(pairs) for b in across] + [(last, b) for b in beside]
 
     def scatter(t, d):
@@ -406,15 +411,36 @@
             one = part[x * rows:(x + 1) * rows]
             part_f32[t, x] = one
             part_send[t, x] = one.astype(jnp.bfloat16)
-        for d in range(1, nx):
-            scatter(t, d)
-        if e >= 4:
-            reduce(e - 4)
-    for e in range(nb - 4, nb):
-        reduce(e)
+        straight = is_end & (t == opposite)
+
+        @pl.when(straight)
+        def _():
+            for x in range(nx):
+                pltpu.make_async_remote_copy(
+                    src_ref=part_send.at[t, x], dst_ref=direct_got.at[me_x],
+                    send_sem=d_sent, recv_sem=d_came, **there(opposite, x)).start()
+
+        @pl.when(jnp.logical_not(straight))
+        def _():
+            for d in range(1, nx):
+                scatter(t, d)
+    for e in range(nb):
+        when(jnp.logical_not(is_end & (order_here(e) == opposite)), lambda: reduce(e))
 
     with jax.named_scope("wF"):
-        await_bytes(out_ref.at[pl.ds(0, nb - 1)], f_came)
+        @pl.when(is_end)
+        def _():
+            await_bytes(direct_got, d_came)
+            total = direct_got[0].astype(jnp.float32)
+            for x in range(1, nx):
+                total += direct_got[x].astype(jnp.float32)
+            out_ref[opposite] = (gain_ref[opposite] * total).astype(jnp.bfloat16)
+            if nb > 2:
+                await_bytes(out_ref.at[pl.ds(0, nb - 2)], f_came)
+
+        @pl.when(jnp.logical_not(is_end))
+        def _():
+            await_bytes(out_ref.at[pl.ds(0, nb - 1)], f_came)
 
     with jax.named_scope("drain"):
         w_swap.wait_send()
@@ -426,8 +452,17 @@
         def _():
             await_bytes(att.at[:, pl.ds(0, side * (side - 1))], passed)
 
-        await_bytes(part_send.at[:, pl.ds(0, nx - 1)], r_sent)
-        await_bytes(final_send.at[pl.ds(0, nb - 1)], f_sent)
+        @pl.when(is_end)
+        def _():
+            await_bytes(part_send.at[0], d_sent)
+            await_bytes(part_send.at[pl.ds(0, nb - 1), pl.ds(0, nx - 1)], r_sent)
+            if nb > 2:
+                await_bytes(final_send.at[pl.ds(0, nb - 2)], f_sent)
+
+        @pl.when(jnp.logical_not(is_end))
+        def _():
+            await_bytes(part_send.at[:, pl.ds(0, nx - 1)], r_sent)
+            await_bytes(final_send.at[pl.ds(0, nb - 1)], f_sent)
 
 
 def fused(nb, nu, query, keys, values, out_weight, out_gain):
@@ -458,9 +493,10 @@
             vmem((nb, nx, rows, columns), bf16),
             vmem((nb, nx, rows, columns), bf16),
             vmem((nb, rows, columns), bf16),
+            vmem((nx, rows, columns), bf16),
             dma, dma, dma, dma, dma, dma((pairs,)), dma, dma((pairs,)),
             pltpu.SemaphoreType.REGULAR((nb - 1,)),
-            dma, dma((pairs, nb)), dma((nb, nb)), dma, dma, dma((nb, nx - 1)), dma, dma,
+            dma, dma((pairs, nb)), dma((nb, nb)), dma, dma, dma((nb, nx - 1)), dma, dma, dma, dma,
         ],
         compiler_params=pltpu.CompilerParams(
             collective_id=0, has_side_effects=True),

time: 33.6 us -> 33 us (0.982)
  Pallas kernels: 32.8 us -> 32.1 us
    pallas_call x1, Pallas kernels: 32.8 us -> 32.1 us  [fused(): pl.pallas_call(functools.partial(attend_kernel, nb, nu), out_shape=vmem((...]
where the time goes in v6:
time: 33 us; the launch traced here: 32.8 us
  Pallas kernels  32.1 us (97%)
  local copies, waits for them, and re-layouts  0.67 us (2%)
    pallas_call x1, Pallas kernels, fused(): pl.pallas_call(functools.partial(attend_kernel, nb, nu), out_shape=vmem((...  32.1 us
    reshape x1, local copies, waits for them, and re-layouts, fused(): return gathered.transpose(1, 0, 2).reshape(rows, width)  0.67 us

profile of v6, /device:TPU:0, one launch (start us, length us, event | category | flops | bytes accessed | tf_op | source)
XLA Modules:
  0.0 32.8 jit_solution(657092987521998114)
XLA Ops:
  0.0 32.1 %shard_map.55 = bf16[4,24,768]{2,1,0:T(8,128)(2,1)S(1)} custom-call(bf16[24,3072]{1,0:T(8,128)(2,1)} %q_hbm.1, bf16[24,3072]{1,0:T(8,128)(2,1)} %k_hbm.1, bf16[24,3072]{1,0:T(8,128)(2,1)} %v_hbm.1, bf16[768,768]{1,0:T(8,128)(2,1)} %w_hbm.1, f32[4,1,768]{2,1,0:T(1,128)} %bitcast.5), custom_call_target="tpu_custom_call" | custom-call | tf_op jit(solution)/shard_map/pallas_call | solution.py:478
  32.1 0.7 %copy.7 = bf16[4,3,8,768]{3,2,0,1:T(8,128)(2,1)} copy(bf16[4,3,8,768]{3,2,1,0:T(8,128)(2,1)S(1)} %bitcast.4) | data formatting | bytes 294912 | tf_op jit(solution)/shard_map/reshape | solution.py:504

commit v7 on v6

--- a/solution.py
+++ b/solution.py
@@ -114,7 +114,7 @@
     gate_here = (side - 1) + my_side
     gate_there = side - my_side
     is_gate = me_b == gate_here
-    held = me_b < 0
+    held = (me_b < side) & jnp.logical_not(is_gate) & (lax.rem(me_u, 2) == 1)
     far_side = (1 - my_side) * side
 
     def turn_of(b, e):
@@ -252,6 +252,20 @@
         for d in range(1, side):
             spread(p, d)
 
+    def spread_near_turn(e):
+        for d in range(1, side):
+            t = turn_of(target(d), e)
+            push(last, d, me_b, t, b_sent, came(last, me_b, t))
+
+    def near_rest():
+        for e in range(1, nb):
+            spread_near_turn(e)
+
+    columns = w_hbm.shape[1]
+
+    def column(b):
+        return out_ref.at[:, pl.ds(pl.multiple_of(b * columns, LANES), columns)]
+
     def far_of(i):
         return far_side + my_side * i + (1 - my_side) * (side - 1 - i)
 
@@ -259,7 +273,7 @@
         return my_side * side + lax.rem(me_b + d, side)
 
     upper = my_side == 1
-    late_core = (me_b < side) & (me_c == 1)
+    late_core = is_gate & (me_c == 1)
 
     def forward(p, turns, whose, fresh=True, only=True):
         @pl.when(is_gate & only)
@@ -354,10 +368,14 @@
                                 forward(early, head, [i], only=jnp.logical_not(upper))
                             else:
                                 forward(early, head, [i])
-                spread_near(p)
+                spread_near_turn(0)
+                when(my_side == 0, near_rest)
                 fill_early()
-                with jax.named_scope(f"fwl"):
-                    forward(last, head, every)
+                with jax.named_scope("fwl"):
+                    forward(last, head[:1], every)
+                when(my_side == 1, near_rest)
+                with jax.named_scope("fwk"):
+                    forward(last, head[1:], every)
                 for early in range(last):
                     forward(early, tail, every, fresh=False)
                 with jax.named_scope(f"fwm"):
@@ -383,13 +401,13 @@
 
         @pl.when(me_b == t)
         def _():
-            out_ref[t] = gated
+            out_ref[:, pl.ds(pl.multiple_of(t * columns, LANES), columns)] = gated
 
         @pl.when(me_b != t)
         def _():
             final_send[t] = gated
             pltpu.make_async_remote_copy(
-                src_ref=final_send.at[t], dst_ref=out_ref.at[me_b],
+                src_ref=final_send.at[t], dst_ref=column(me_b),
                 send_sem=f_sent, recv_sem=f_came, **there(t, me_x)).start()
 
     for e in range(nb):
@@ -434,13 +452,14 @@
             total = direct_got[0].astype(jnp.float32)
             for x in range(1, nx):
                 total += direct_got[x].astype(jnp.float32)
-            out_ref[opposite] = (gain_ref[opposite] * total).astype(jnp.bfloat16)
+            out_ref[:, pl.ds(pl.multiple_of(opposite * columns, LANES), columns)] = (
+                gain_ref[opposite] * total).astype(jnp.bfloat16)
             if nb > 2:
-                await_bytes(out_ref.at[pl.ds(0, nb - 2)], f_came)
+                await_bytes(out_ref.at[:, pl.ds(0, (nb - 2) * columns)], f_came)
 
         @pl.when(jnp.logical_not(is_end))
         def _():
-            await_bytes(out_ref.at[pl.ds(0, nb - 1)], f_came)
+            await_bytes(out_ref.at[:, pl.ds(0, (nb - 1) * columns)], f_came)
 
     with jax.named_scope("drain"):
         w_swap.wait_send()
@@ -477,7 +496,7 @@
     block = nx * rows
     gathered = pl.pallas_call(
         functools.partial(attend_kernel, nb, nu),
-        out_shape=vmem((nb, rows, columns), bf16),
+        out_shape=vmem((rows, nb * columns), bf16),
         in_specs=[in_hbm] * 5,
         out_specs=pl.BlockSpec(memory_space=pltpu.VMEM),
         scratch_shapes=[
@@ -501,7 +520,7 @@
         compiler_params=pltpu.CompilerParams(
             collective_id=0, has_side_effects=True),
     )(query, keys, values, out_weight, out_gain.reshape(nb, 1, columns))
-    return gathered.transpose(1, 0, 2).reshape(rows, width)
+    return gathered
 
 
 def on_any(nb, nu, query, keys, values, out_weight, out_gain):

time: 33 us -> 32.4 us (0.982)
  Pallas kernels: 32.1 us -> 31.6 us
    reshape x1 -> x0, local copies, waits for them, and re-layouts: 0.67 us -> none  [fused(): return gathered.transpose(1, 0, 2).reshape(rows, width)]
    unnamed x0 -> x1, local copies, waits for them, and re-layouts: none -> 0.66 us
    pallas_call x1, Pallas kernels: 32.1 us -> 31.6 us  [fused(): pl.pallas_call(functools.partial(attend_kernel, nb, nu), out_shape=vmem((...]
where the time goes in v7:
time: 32.4 us; the launch traced here: 32.3 us
  Pallas kernels  31.6 us (98%)
  local copies, waits for them, and re-layouts  0.66 us (2%)
    pallas_call x1, Pallas kernels, fused(): pl.pallas_call(functools.partial(attend_kernel, nb, nu), out_shape=vmem((...  31.6 us
    unnamed x1, local copies, waits for them, and re-layouts  0.66 us

profile of v7, /device:TPU:0, one launch (start us, length us, event | category | flops | bytes accessed | tf_op | source)
XLA Modules:
  0.0 32.3 jit_solution(16091062539132979400)
XLA Ops:
  0.0 31.6 %shard_map.55 = bf16[24,3072]{1,0:T(8,128)(2,1)S(1)} custom-call(bf16[24,3072]{1,0:T(8,128)(2,1)} %q_hbm.1, bf16[24,3072]{1,0:T(8,128)(2,1)} %k_hbm.1, bf16[24,3072]{1,0:T(8,128)(2,1)} %v_hbm.1, bf16[768,768]{1,0:T(8,128)(2,1)} %w_hbm.1, f32[4,1,768]{2,1,0:T(1,128)} %bitcast.1), custom_call_target="tpu_custom_call" | custom-call | tf_op jit(solution)/shard_map/pallas_call | solution.py:497
  31.6 0.7 %copy.7 = bf16[24,3072]{1,0:T(8,128)(2,1)} copy(bf16[24,3072]{1,0:T(8,128)(2,1)S(1)} %shard_map.55) | data formatting | bytes 294912

commit v8 on v7

--- a/solution.py
+++ b/solution.py
@@ -229,8 +229,9 @@
     def target(d):
         return gate_there if d == 0 else my_side * side + lax.rem(me_b + d, side)
 
-    def came(p, b, t):
-        return b_came.at[p, b] if t is None else b_last.at[b, t]
+    def came(p, b, t, taker):
+        slot = b - (b > taker)
+        return b_came.at[p, slot] if t is None else b_last.at[slot, t]
 
     def piece(p, b, t):
         return att.at[p, b] if t is None else att.at[p, b, t]
@@ -242,11 +243,11 @@
 
     def spread(p, d):
         if p < last:
-            push(p, d, me_b, None, b_sent, came(p, me_b, None))
+            push(p, d, me_b, None, b_sent, came(p, me_b, None, target(d)))
         else:
             for e in range(nb):
                 t = turn_of(target(d), e)
-                push(p, d, me_b, t, b_sent, came(p, me_b, t))
+                push(p, d, me_b, t, b_sent, came(p, me_b, t, target(d)))
 
     def spread_near(p):
         for d in range(1, side):
@@ -255,7 +256,7 @@
     def spread_near_turn(e):
         for d in range(1, side):
             t = turn_of(target(d), e)
-            push(last, d, me_b, t, b_sent, came(last, me_b, t))
+            push(last, d, me_b, t, b_sent, came(last, me_b, t, target(d)))
 
     def near_rest():
         for e in range(1, nb):
@@ -283,11 +284,11 @@
                 for i in whose:
                     b = far_of(i)
                     if p == last:
-                        await_bytes(att.at[p, b, t], b_last.at[b, t])
+                        await_bytes(att.at[p, b, t], came(last, b, t, me_b))
                     elif fresh and e == turns[0]:
-                        await_bytes(att.at[p, b], b_came.at[p, b])
+                        await_bytes(att.at[p, b], came(p, b, None, me_b))
                     for d in range(1, side):
-                        push(p, d, b, t, passed, came(p, b, t))
+                        push(p, d, b, t, passed, came(p, b, t, target(d)))
 
     every = list(range(side))
     head, tail = range(nb - 1), range(nb - 1, nb)
@@ -304,7 +305,7 @@
         for p in range(last):
             for d in range(1, side):
                 with jax.named_scope(f"wB{p}"):
-                    await_bytes(att.at[p, beside[d]], b_came.at[p, beside[d]])
+                    await_bytes(att.at[p, beside[d]], came(p, beside[d], None, me_b))
         if last:
             early = [(p, b) for p in range(last) for b in beside]
             seen = jnp.concatenate([att[p, b].reshape(mine_rows, LANES) for p, b in early], axis=1)
@@ -416,10 +417,10 @@
             @pl.when(jnp.logical_not(is_gate))
             def _():
                 for b in across:
-                    await_bytes(att.at[:, b, t], b_last.at[b, t])
+                    await_bytes(att.at[:, b, t], came(last, b, t, me_b))
 
             for d in range(1, side):
-                await_bytes(att.at[last, beside[d], t], b_last.at[beside[d], t])
+                await_bytes(att.at[last, beside[d], t], came(last, beside[d], t, me_b))
         seen = jnp.concatenate([att[p, b, t] for p, b in late], axis=1)
         weight = jnp.concatenate([weight_of(p, b) for p, b in late], axis=0)
         part = jnp.dot(seen, weight, preferred_element_type=jnp.float32)
@@ -515,7 +516,7 @@
             vmem((nx, rows, columns), bf16),
             dma, dma, dma, dma, dma, dma((pairs,)), dma, dma((pairs,)),
             pltpu.SemaphoreType.REGULAR((nb - 1,)),
-            dma, dma((pairs, nb)), dma((nb, nb)), dma, dma, dma((nb, nx - 1)), dma, dma, dma, dma,
+            dma, dma((max(pairs - 1, 1), nb - 1)), dma((nb - 1, nb)), dma, dma, dma((nb, nx - 1)), dma, dma, dma, dma,
         ],
         compiler_params=pltpu.CompilerParams(
             collective_id=0, has_side_effects=True),

time: 32.4 us -> 32.4 us (level)
  no operation moved by 1% of the time
where the time goes in v8:
time: 32.4 us; the launch traced here: 32.2 us
  Pallas kernels  31.5 us (97%)
  local copies, waits for them, and re-layouts  0.66 us (2%)
    pallas_call x1, Pallas kernels, fused(): pl.pallas_call(functools.partial(attend_kernel, nb, nu), out_shape=vmem((...  31.5 us
    unnamed x1, local copies, waits for them, and re-layouts  0.66 us

profile of v8, /device:TPU:0, one launch (start us, length us, event | category | flops | bytes accessed | tf_op | source)
XLA Modules:
  0.0 32.2 jit_solution(211968468544346156)
XLA Ops:
  0.0 31.5 %shard_map.55 = bf16[24,3072]{1,0:T(8,128)(2,1)S(1)} custom-call(bf16[24,3072]{1,0:T(8,128)(2,1)} %q_hbm.1, bf16[24,3072]{1,0:T(8,128)(2,1)} %k_hbm.1, bf16[24,3072]{1,0:T(8,128)(2,1)} %v_hbm.1, bf16[768,768]{1,0:T(8,128)(2,1)} %w_hbm.1, f32[4,1,768]{2,1,0:T(1,128)} %bitcast.1), custom_call_target="tpu_custom_call" | custom-call | tf_op jit(solution)/shard_map/pallas_call | solution.py:498
  31.5 0.7 %copy.7 = bf16[24,3072]{1,0:T(8,128)(2,1)} copy(bf16[24,3072]{1,0:T(8,128)(2,1)S(1)} %shard_map.55) | data formatting | bytes 294912
